TPU v7x, 256 devices: a whole 4x4x8 slice. The times are simulated.
256 devices in a mesh: dp: 8 (over z), expert: 8 (over x, y_lo), shard: 4 (over y_hi, core).
Axes of the slice: x: 4, y: 4 (y_hi: 2, y_lo: 2; y = y_hi * 2 + y_lo), z: 8, core: 2. Of those that a mesh axis runs over, the one named last changes fastest.
Arguments:
- activations: bfloat16 [2, 8, 4096, 256], P(None, 'expert', ('dp', 'shard')), may hold values from -6 to 6
- out_grads: bfloat16 [2, 8, 4096, 14336], P(None, 'expert', ('dp', 'shard')), may hold values from -0.25 to 0.25
- weights: float32 [2, 8, 256, 14336], P(None, 'expert', ('dp', 'shard')), may hold values from -4 to 4
- shadow: float32 [2, 8, 256, 14336], P(None, 'expert', ('dp', 'shard')), may hold values from -4 to 4
- counts: int32 [2, 256, 8], P(None, ('dp', 'expert', 'shard')), may hold values from 1 to 1024, as said below
Outputs:
- new_weights: float32 [2, 8, 256, 14336], P(None, 'expert', ('dp', 'shard'))
- new_shadow: float32 [2, 8, 256, 14336], P(None, 'expert', ('dp', 'shard'))
Inputs may be any that keep to these rules, and one draw needn't show every extreme that they name: `counts`: loads differ between the experts of a layer.
All inputs are finite; a program needn't handle non-finite values.
Results may differ from a plain program's by a relative error of at most 0.0003.
Values sent between devices are 32-bit elements; how exact they have to be, the bound alone decides.
A program may use at most 128 MiB of HBM per device.

v0:
```python
from functools import partial

import jax
import jax.numpy as jnp
from jax import lax
from jax.sharding import Mesh
from jax.sharding import PartitionSpec as P

LAYERS = 2
EXPERT = ("expert_0", "expert_1")
DP_EXPERT_SHARD = ("dp", "expert_0", "expert_1", "shard_0", "shard_1")
DP_SHARD = ("dp", "shard_0", "shard_1")


step_size = 0.5
clip_level = 1.0


def by_axis(value, axes):
    for axis in axes:
        value = lax.psum(value, axis)
    return value


def sent_to_all(value, axis):
    copies = jnp.broadcast_to(value, (lax.axis_size(axis), *value.shape))
    return lax.all_to_all(copies, axis, split_axis=0, concat_axis=0, tiled=True)


def taken_together(value, axis):
    return sent_to_all(value, axis).sum(axis=0)


def partial_rows(inputs, cotangent, start, count):
    return lax.dot_general(
        inputs, cotangent, (((0,), (0,)), ((), ())), preferred_element_type=jnp.float32
    )


def on_device(activations, out_grads, weights, shadow, counts):
    experts = counts.shape[-1]
    own_slot = (jnp.arange(experts) == lax.axis_index(EXPERT)).astype(jnp.float32)
    own_rows = weights.shape[2]
    load_totals = by_axis(counts[:, 0, :], DP_EXPERT_SHARD)
    all_weights = []
    all_shadow = []
    for layer_index in range(LAYERS):
        inputs = activations[layer_index, 0]
        cotangent = out_grads[layer_index, 0]
        term = partial(partial_rows, inputs, cotangent)
        summed = lax.psum_scatter(
            term(jnp.int32(0), lax.axis_size(DP_SHARD) * own_rows),
            DP_SHARD,
            scatter_dimension=0,
            tiled=True,
        )
        squares = jnp.sum(summed * summed)
        loads = load_totals[layer_index].astype(jnp.float32)
        total_squares = taken_together(squares, DP_SHARD)
        own_load = jnp.sum(loads * own_slot)
        mean_load = jnp.mean(loads)
        numel = inputs.shape[1] * cotangent.shape[1]
        root_mean = jnp.sqrt(total_squares / numel)
        factor = (
            step_size * (own_load / mean_load) * clip_level / jnp.maximum(root_mean, clip_level)
        )
        updated = weights[layer_index, 0] - factor * summed
        beta = own_load / (own_load + mean_load)
        previous = shadow[layer_index, 0]
        all_weights.append(updated)
        all_shadow.append(previous + beta * (updated - previous))
    return (jnp.stack(all_weights)[:, None], jnp.stack(all_shadow)[:, None])


def solution(mesh):
    split = Mesh(
        mesh.devices.reshape(mesh.shape["dp"], 4, 2, 2, 2),
        ("dp", "expert_0", "expert_1", "shard_0", "shard_1"),
    )
    return jax.shard_map(
        on_device,
        mesh=split,
        in_specs=(
            P(None, EXPERT, DP_SHARD, None),
            P(None, EXPERT, DP_SHARD, None),
            P(None, EXPERT, DP_SHARD, None),
            P(None, EXPERT, DP_SHARD, None),
            P(None, DP_EXPERT_SHARD, None),
        ),
        out_specs=(P(None, EXPERT, DP_SHARD, None), P(None, EXPERT, DP_SHARD, None)),
        check_vma=False,
    )
```

profile of v0, /device:TPU:1, one launch (start us, length us, event | category | flops | bytes accessed | tf_op | source)
XLA Modules:
  0.0 422.3 jit_solution(12964955287590838810)
XLA Ops:
  7.2 9.4 %fusion = f32[256,14336]{1,0:T(8,128)} fusion(bf16[2,1,128,14336]{3,2,1,0:T(8,128)(2,1)} %param.6, bf16[2,1,128,256]{3,2,1,0:T(8,128)(2,1)} %param.5), kind=kOutput, calls=%fused_computation | convolution fusion | flops 939524096 | bytes 18415616 | tf_op jit(solution)/shard_map/dot_general | solution.py:35
  16.7 0.8 copy-done.2
  17.5 9.3 %fusion.2 = f32[256,14336]{1,0:T(8,128)} fusion(bf16[2,1,128,14336]{3,2,1,0:T(8,128)(2,1)} %param.6, bf16[2,1,128,256]{3,2,1,0:T(8,128)(2,1)S(1)} %copy-done.2), kind=kOutput, calls=%fused_computation.2 | convolution fusion | flops 939524096 | bytes 18415616 | tf_op jit(solution)/shard_map/dot_general | solution.py:35
  26.9 0.6 copy-done.3
  27.5 14.0 %psum.35 = s32[2,8]{1,0:T(2,128)S(1)} all-reduce(s32[2,8]{1,0:T(2,128)S(1)} %bitcast.63), channel_id=1, replica_groups=mesh['dp'=8,'expert_0'=4,'expert_1'=2,'shard_0'=2,'shard_1'=2] {'dp'}, use_global_device_ids=true, to_apply=%region_0.0 | all-reduce | flops 16 | bytes 128 | tf_op jit(solution)/shard_map/psum | solution.py:21
  41.5 6.9 %psum.36 = s32[2,8]{1,0:T(2,128)S(1)} all-reduce(s32[2,8]{1,0:T(2,128)S(1)} %psum.35), channel_id=1, replica_groups=mesh['dp'=8,'expert_0'=4,'expert_1'=2,'shard_0'=2,'shard_1'=2] {'expert_0'}, use_global_device_ids=true, to_apply=%region_1.0 | all-reduce | flops 16 | bytes 128 | tf_op jit(solution)/shard_map/psum | solution.py:21
  48.5 3.1 psum.37
  51.6 4.7 %psum.38 = s32[2,8]{1,0:T(2,128)S(1)} all-reduce(s32[2,8]{1,0:T(2,128)S(1)} %psum.37), channel_id=1, replica_groups=mesh['dp'=8,'expert_0'=4,'expert_1'=2,'shard_0'=2,'shard_1'=2] {'shard_0'}, use_global_device_ids=true, to_apply=%region_3.0 | all-reduce | flops 16 | bytes 128 | tf_op jit(solution)/shard_map/psum | solution.py:21
  56.3 9.2 %psum.39 = s32[2,8]{1,0:T(2,128)S(1)} all-reduce(s32[2,8]{1,0:T(2,128)S(1)} %psum.38), channel_id=1, replica_groups=mesh['dp'=8,'expert_0'=4,'expert_1'=2,'shard_0'=2,'shard_1'=2] {'shard_1'}, use_global_device_ids=true, to_apply=%region_4.0 | all-reduce | flops 16 | bytes 128 | tf_op jit(solution)/shard_map/psum | solution.py:21
  65.5 0.6 convert_reduce_fusion.1
  66.7 0.6 fusion.16
  71.8 129.3 %reduce-scatter.5.cloned.1.call-done = f32[8,14336]{1,0:T(8,128)} async-done(((f32[256,14336]{1,0:T(8,128)}), f32[8,14336]{1,0:T(8,128)}) %reduce-scatter.5.cloned.1.call-update) | async-done | bytes 458768 | tf_op jit(solution)/shard_map/reduce_scatter | solution.py:51
  201.1 1.7 multiply_reduce_fusion
  202.9 1.3 broadcast_in_dim.13
  204.1 10.5 %all-to-all-start.1 = ((f32[32,1,1]{2,1,0:T(1,128)}), f32[32,1,1]{2,1,0:T(1,128)S(1)}, u32[]{:S(2)}, u32[]{:S(2)}) async-start(f32[32,1,1]{2,1,0:T(1,128)} %broadcast_in_dim.13), calls=%async_computation.3 | async-start | bytes 32768 | tf_op jit(solution)/shard_map/all_to_all | solution.py:27
  214.7 173.7 %reduce-scatter.3.cloned.1.call-done = f32[8,14336]{1,0:T(8,128)} async-done(((f32[256,14336]{1,0:T(8,128)}), f32[8,14336]{1,0:T(8,128)}) %reduce-scatter.3.cloned.1.call-update) | async-done | bytes 458768 | tf_op jit(solution)/shard_map/reduce_scatter | solution.py:51
  388.4 1.7 multiply_reduce_fusion.1
  390.1 1.3 broadcast_in_dim.12
  391.4 10.6 %all-to-all-start = ((f32[32,1,1]{2,1,0:T(1,128)}), f32[32,1,1]{2,1,0:T(1,128)S(1)}, u32[]{:S(2)}, u32[]{:S(2)}) async-start(f32[32,1,1]{2,1,0:T(1,128)} %broadcast_in_dim.12), calls=%async_computation.1 | async-start | bytes 32768 | tf_op jit(solution)/shard_map/all_to_all | solution.py:27
  402.0 0.6 reduce_sum.79
  403.3 8.0 %all-to-all-done = f32[32,1,1]{2,1,0:T(1,128)S(1)} async-done(((f32[32,1,1]{2,1,0:T(1,128)}), f32[32,1,1]{2,1,0:T(1,128)S(1)}, u32[]{:S(2)}, u32[]{:S(2)}) %all-to-all-start) | async-done | bytes 160 | tf_op jit(solution)/shard_map/all_to_all | solution.py:27
  411.3 0.6 reduce_sum.75
  412.8 1.3 fusion.9
  414.1 1.4 maximum_bitcast_fusion
  (11 shorter events, 0.1 us)
Async XLA Ops:
  7.2 194.0 %reduce-scatter.5.cloned.1.call-start = ((), (), s32[]{:S(2)}) async-start(), calls=%async_computation.5 | async-start | bytes 15138816 | tf_op jit(solution)/shard_map/reduce_scatter | solution.py:51
  16.6 0.9 copy-start.2
  16.6 371.8 %reduce-scatter.3.cloned.1.call-start = ((), (), s32[]{:S(2)}) async-start(), calls=%async_computation.4 | async-start | bytes 15138816 | tf_op jit(solution)/shard_map/reduce_scatter | solution.py:51
  26.8 0.7 copy-start.3
  26.8 385.9 %copy-start = (f32[2,1,8,14336]{3,2,1,0:T(8,128)S(1)}, f32[2,1,8,14336]{3,2,1,0:T(8,128)}, u32[]{:S(2)}) copy-start(f32[2,1,8,14336]{3,2,1,0:T(8,128)} %param.8) | copy-start | bytes 2752516
  26.8 385.9 %copy-start.1 = (f32[2,1,8,14336]{3,2,1,0:T(8,128)S(1)}, f32[2,1,8,14336]{3,2,1,0:T(8,128)}, u32[]{:S(2)}) copy-start(f32[2,1,8,14336]{3,2,1,0:T(8,128)} %param.7) | copy-start | bytes 2752516
  204.1 186.0 %all-to-all-start.1 = ((f32[32,1,1]{2,1,0:T(1,128)}), f32[32,1,1]{2,1,0:T(1,128)S(1)}, u32[]{:S(2)}, u32[]{:S(2)}) async-start(f32[32,1,1]{2,1,0:T(1,128)} %broadcast_in_dim.13), calls=%async_computation.3 | async-start | bytes 32768 | tf_op jit(solution)/shard_map/all_to_all | solution.py:27
  391.4 19.9 %all-to-all-start = ((f32[32,1,1]{2,1,0:T(1,128)}), f32[32,1,1]{2,1,0:T(1,128)S(1)}, u32[]{:S(2)}, u32[]{:S(2)}) async-start(f32[32,1,1]{2,1,0:T(1,128)} %broadcast_in_dim.12), calls=%async_computation.1 | async-start | bytes 32768 | tf_op jit(solution)/shard_map/all_to_all | solution.py:27
Sparse Core Ops, SparseCore 0:
  16.8 184.3 reduce-scatter.4
  205.7 182.6 reduce-scatter.2
where the time goes:
time: 423 us; the launch traced here: 422 us
  waiting for transfers between devices  311 us (74%)
  blocking collectives  37.9 us (9%)
  starting transfers between devices  21.2 us (5%)
  between operations  20.7 us (5%)
  matrix products  18.7 us (4%)
  other arithmetic  8.65 us (2%)
    reduce_scatter x2, waiting for transfers between devices, on_device(): lax.psum_scatter(term(jnp.int32(0), lax.axis_size(DP_SHARD) * own_rows),...  303 us
    psum x5, blocking collectives, by_axis(): value = lax.psum(value, axis)  37.9 us
    all_to_all x2, starting transfers between devices, sent_to_all(): return lax.all_to_all(copies, axis, split_axis=0, concat_axis=0, tiled=True)  21.2 us
    dot_general x2, matrix products, partial_rows(): lax.dot_general(inputs, cotangent, (((0,), (0,)), ((), ())), preferred_el...  18.7 us
  transfers between devices with their start and end apart: 4, of which 3 were waited for; matrix products, arithmetic and copies ran while one was open for 4% of the time, Pallas kernels for 0%

commit v1 on v0

v1 whole, which is shorter than its diff:
```python
import functools

import jax
import jax.numpy as jnp
from jax import lax
from jax.experimental import pallas as pl
from jax.experimental.pallas import tpu as pltpu
from jax.sharding import Mesh
from jax.sharding import PartitionSpec as P

MESH = pl.DeviceIdType.MESH
LAYERS = 2
EXPERT = ("expert_0", "expert_1")
DP_EXPERT_SHARD = ("dp", "expert_0", "expert_1", "shard_0", "shard_1")
DP_SHARD = ("dp", "shard_0", "shard_1")

step_size = 0.5
clip_level = 1.0

NZ = 8
BLOCKS = 8
ZF = 4


def kernel(
    acts, og, counts, grad, factor_out, beta_out,
    part, ring, y_got, y_relay, z_got, z_relay, x_got, x_out, own_half, other_half,
    a_out, a_got, a_rows, a_t, gbuf, c_own, c_got, d_own, d_got, q_own, q_got, q_acc,
    og_sem, x_send, x_recv, a_sem, ring_send, ring_recv, y_sem, z_sem, g_sem, c_sem, d_sem, q_sem, out_sem,
):
    z = lax.axis_index("dp")
    x = lax.axis_index("expert_0")
    y_lo = lax.axis_index("expert_1")
    y_hi = lax.axis_index("shard_0")
    core = lax.axis_index("shard_1")
    y = y_hi * 2 + y_lo
    tokens = acts.shape[1]
    rows = acts.shape[2]
    half_rows = rows // 2
    unit = half_rows // NZ
    width = part.shape[-1]
    own_rows = unit // 2
    half_cols = BLOCKS * width

    def at(z=z, x=x, y_lo=y_lo, y_hi=y_hi, core=core):
        return (z, x, y_lo, y_hi, core)

    def z_next(sign):
        return at(z=lax.rem(z + sign + NZ, NZ))

    def y_next(sign):
        to = lax.rem(y + sign + 4, 4)
        return at(y_lo=lax.rem(to, 2), y_hi=to // 2)

    mate = at(core=1 - core)
    me_group = z * 4 + y_hi * 2 + core
    me_expert = x * 2 + y_lo

    def group_device(offset):
        to = lax.rem(me_group + offset, 32)
        return at(z=to // 4, y_hi=lax.rem(to // 2, 2), core=lax.rem(to, 2))

    def expert_device(offset):
        to = lax.rem(me_expert + offset, 8)
        return at(x=to // 2, y_lo=lax.rem(to, 2))

    def remote(src, dst, send, recv, device):
        return pltpu.make_async_remote_copy(
            src_ref=src, dst_ref=dst, send_sem=send, recv_sem=recv, device_id=device, device_id_type=MESH
        )

    def og_copy(layer, which, b):
        first = core if which == 0 else 1 - core
        to = own_half if which == 0 else other_half
        cols = pl.ds(pl.multiple_of(first * half_cols + b * width, 128), width)
        return pltpu.make_async_copy(og.at[layer, :, cols], to.at[layer, b], og_sem.at[layer, which, b])

    for layer in range(LAYERS):
        def start(b, _):
            og_copy(layer, 1, b).start()
            og_copy(layer, 0, b).start()
            return 0
        lax.fori_loop(0, BLOCKS, start, 0)

    barrier = pltpu.get_barrier_semaphore()

    def greet_group(offset, _):
        pl.semaphore_signal(barrier, inc=1, device_id=group_device(offset), device_id_type=MESH)
        return 0

    def greet_expert(offset, _):
        pl.semaphore_signal(barrier, inc=1, device_id=expert_device(offset), device_id_type=MESH)
        return 0

    lax.fori_loop(1, 32, greet_group, 0)
    lax.fori_loop(1, 8, greet_expert, 0)
    pl.semaphore_signal(barrier, inc=1, device_id=at(y_lo=1 - y_lo, y_hi=1 - y_hi), device_id_type=MESH)

    a_out[...] = acts[...].astype(jnp.float32)
    c_own[...] = jnp.zeros_like(c_own)
    c_own[:, 0:8] = counts[:, 0, :].astype(jnp.float32)
    q_acc[...] = jnp.zeros_like(q_acc)

    def convert(layer, b):
        og_copy(layer, 1, b).wait()
        x_out[b] = other_half[layer, b].astype(jnp.float32)

    def x_copy(layer, b):
        return remote(x_out.at[b], x_got.at[layer, b], x_send.at[b], x_recv.at[layer, b], mate)

    convert(0, 0)
    pl.semaphore_wait(barrier, 39)

    a_copy = remote(a_out, a_got, a_sem.at[0], a_sem.at[1], mate)
    a_copy.start()

    def swap(b, _):
        convert(0, b)
        x_copy(0, b).start()
        return 0

    x_copy(0, 0).start()
    lax.fori_loop(1, BLOCKS, swap, 0)

    def c_copy(offset):
        return remote(c_own, c_got.at[offset - 1], c_sem.at[0, offset - 1], c_sem.at[1, offset - 1], expert_device(offset))

    def each(copy, low, high, what):
        def body(i, _):
            getattr(copy(i), what)()
            return 0
        lax.fori_loop(low, high, body, 0)

    a_copy.wait_recv()
    for layer in range(LAYERS):
        a_rows[:, 0:tokens] = a_out[layer].T
        a_rows[:, tokens : 2 * tokens] = a_got[layer].T
        for half in range(2):
            side = y_hi if half == 0 else 1 - y_hi
            for zz in range(NZ):
                piece = a_rows[pl.ds(pl.multiple_of(zz * 2 * unit + side * unit, unit), unit), :]
                a_t[layer, half * half_rows + zz * unit : half * half_rows + (zz + 1) * unit, :] = piece.astype(jnp.bfloat16)

    def multiply(layer, b):
        x_copy(layer, b).wait_recv()
        og_copy(layer, 0, b).wait()
        both = jnp.concatenate([own_half[layer, b], x_got[layer, b].astype(jnp.bfloat16)], axis=0)
        part[layer, b] = jnp.dot(a_t[layer], both, preferred_element_type=jnp.float32)

    def stream(phase, slot):
        if phase < 2:
            return phase, slot // 2, lax.rem(slot, 2)
        return slot // 4, ZF + lax.rem(slot, 4), 0

    def sign_of(b):
        return 1 - 2 * lax.rem(b, 2)

    def chunk(layer, b, half, index):
        return part.at[layer, b, pl.ds(pl.multiple_of(half * half_rows + index * unit, unit), unit), :]

    def ring_copy(phase, slot, step):
        layer, b, half = stream(phase, slot)
        sign = sign_of(b)
        k = phase * 8 + slot
        if step == 0:
            src = chunk(layer, b, half, lax.rem(z - sign + NZ, NZ))
        else:
            src = ring.at[k, step - 1]
        return remote(src, ring.at[k, step], ring_send.at[k], ring_recv.at[k, step], z_next(sign))

    def ring_step(phase, slot, step):
        layer, b, half = stream(phase, slot)
        k = phase * 8 + slot
        before = ring_copy(phase, slot, step - 1)
        before.wait_recv()
        index = lax.rem(z - sign_of(b) * (1 + step) + 2 * NZ, NZ)
        ring[k, step - 1] = ring[k, step - 1] + chunk(layer, b, half, index)[...]
        before.wait_send()
        ring_copy(phase, slot, step).start()

    def ring_last(phase, slot):
        layer, b, half = stream(phase, slot)
        k = phase * 8 + slot
        before = ring_copy(phase, slot, NZ - 2)
        before.wait_recv()
        before.wait_send()
        return ring[k, NZ - 2] + chunk(layer, b, half, z)[...]

    def round_of(phase, step, low=0, high=8):
        def body(slot, _):
            ring_step(phase, slot, step)
            return 0
        lax.fori_loop(low, high, body, 0)

    def y_copy(layer, j):
        return remote(
            part.at[layer, ZF + j, pl.ds(half_rows, half_rows), :], y_relay.at[layer, j],
            y_sem.at[0, layer, j], y_sem.at[1, layer, j], y_next(sign_of(j)),
        )

    def y_pass(layer, j):
        return remote(
            y_relay.at[layer, j], y_got.at[layer, j], y_sem.at[2, layer, j], y_sem.at[3, layer, j], y_next(sign_of(j))
        )

    def y_forward(layer, low, high):
        def body(j, _):
            y_copy(layer, j).wait_recv()
            y_pass(layer, j).start()
            return 0
        lax.fori_loop(low, high, body, 0)

    def z_copy(layer, j):
        return remote(
            ring.at[layer * 8 + j * 2 + 1, NZ - 2], z_relay.at[layer, j],
            z_sem.at[0, layer, j], z_sem.at[1, layer, j], y_next(sign_of(j)),
        )

    def z_pass(layer, j):
        return remote(
            z_relay.at[layer, j], z_got.at[layer, j], z_sem.at[2, layer, j], z_sem.at[3, layer, j], y_next(sign_of(j))
        )

    def z_forward(layer):
        def body(j, _):
            z_copy(layer, j).wait_recv()
            z_pass(layer, j).start()
            return 0
        lax.fori_loop(0, ZF, body, 0)

    def gcols(side, b):
        return pl.ds(pl.multiple_of(side * half_cols + b * width, 128), width)

    def g_copy(layer, b, k):
        src = ring.at[k, NZ - 2, pl.ds(pl.multiple_of((1 - core) * own_rows, own_rows), own_rows), :]
        return remote(src, gbuf.at[layer, :, gcols(core, b)], g_sem.at[0, layer, b], g_sem.at[1, layer, b], mate)

    def finish(layer, b, k, value):
        ring[k, NZ - 2] = value
        g_copy(layer, b, k).start()
        gbuf[layer, :, gcols(core, b)] = ring[k, NZ - 2, pl.ds(pl.multiple_of(core * own_rows, own_rows), own_rows), :]
        squares = value * value
        folded = squares[0:own_rows] + squares[own_rows : 2 * own_rows]
        total = folded[:, 0:128]
        for i in range(1, width // 128):
            total = total + folded[:, i * 128 : (i + 1) * 128]
        q_acc[layer] = q_acc[layer] + total

    def zf_end(layer):
        def body(j, _):
            slot = j * 2 + 1
            ring[layer * 8 + slot, NZ - 2] = ring_last(layer, slot)
            z_copy(layer, j).start()
            slot = j * 2
            ring[layer * 8 + slot, NZ - 2] = ring_last(layer, slot)
            return 0
        lax.fori_loop(0, ZF, body, 0)

    def zf_finish(layer):
        def body(j, _):
            z_pass(layer, j).wait_recv()
            k = layer * 8 + j * 2
            finish(layer, j, k, ring[k, NZ - 2] + z_got[layer, j])
            return 0
        lax.fori_loop(0, ZF, body, 0)

    def zf_begin(layer):
        def body(b, _):
            multiply(layer, b)
            return 0
        lax.fori_loop(0, ZF, body, 0)

    def zf_start(phase):
        def body(slot, _):
            ring_copy(phase, slot, 0).start()
            return 0
        lax.fori_loop(0, 8, body, 0)

    def first(b, _):
        multiply(0, b)
        ring_copy(0, b * 2, 0).start()
        ring_copy(0, b * 2 + 1, 0).start()
        return 0

    lax.fori_loop(0, ZF, first, 0)

    def second(j, _):
        multiply(0, ZF + j)
        y_copy(0, j).start()
        return 0

    lax.fori_loop(0, BLOCKS - ZF, second, 0)
    each(c_copy, 1, 8, "start")

    def swap_again(b, _):
        x_copy(0, b).wait_send()
        convert(1, b)
        x_copy(1, b).start()
        return 0

    lax.fori_loop(0, BLOCKS, swap_again, 0)
    round_of(0, 1)

    def more(b, _):
        multiply(1, b)
        return 0

    lax.fori_loop(0, ZF, more, 0)
    round_of(0, 2)
    lax.fori_loop(ZF, BLOCKS, more, 0)
    round_of(0, 3)
    y_forward(0, 0, 2)

    each(c_copy, 1, 8, "wait_recv")
    d_own[...] = c_own[...] + jnp.sum(c_got[...], axis=0)

    def d_copy(offset):
        return remote(d_own, d_got.at[offset - 1], d_sem.at[0, offset - 1], d_sem.at[1, offset - 1], group_device(offset))

    each(d_copy, 1, 32, "start")
    round_of(0, 4)
    round_of(0, 5)
    y_forward(0, 2, 4)
    each(lambda j: y_copy(1, j), 0, 4, "start")
    round_of(0, 6)

    zf_start(1)
    zf_end(0)
    round_of(1, 1)
    round_of(1, 2)
    round_of(1, 3)
    round_of(1, 4)
    y_forward(1, 0, 2)
    round_of(1, 5)
    z_forward(0)
    round_of(1, 6)
    y_forward(1, 2, 4)

    def yf_start(slot, _):
        layer, b, half = stream(2, slot)
        y_pass(layer, b - ZF).wait_recv()
        part[layer, b, 0:half_rows, :] = part[layer, b, 0:half_rows, :] + y_got[layer, b - ZF]
        ring_copy(2, slot, 0).start()
        return 0

    lax.fori_loop(0, 4, yf_start, 0)
    zf_end(1)
    lax.fori_loop(4, 6, yf_start, 0)
    zf_finish(0)
    round_of(2, 1, 0, 6)
    z_forward(1)
    lax.fori_loop(6, 8, yf_start, 0)
    for step in range(2, 7):
        round_of(2, step, 0, 6)
        round_of(2, step - 1, 6, 8)
    zf_finish(1)

    def yf_end(slot, _):
        layer, b, half = stream(2, slot)
        finish(layer, b, 16 + slot, ring_last(2, slot))
        return 0

    lax.fori_loop(0, 6, yf_end, 0)
    round_of(2, 6, 6, 8)
    lax.fori_loop(6, 8, yf_end, 0)

    q_own[...] = jnp.sum(q_acc[...], axis=1)

    def q_copy(offset):
        return remote(q_own, q_got.at[offset - 1], q_sem.at[0, offset - 1], q_sem.at[1, offset - 1], group_device(offset))

    each(q_copy, 1, 32, "start")

    each(d_copy, 1, 32, "wait_recv")
    totals = d_own[...] + jnp.sum(d_got[...], axis=0)
    lanes = lax.broadcasted_iota(jnp.int32, totals.shape, 1)
    mean_load = jnp.sum(totals, axis=1, keepdims=True) / 8.0
    own_load = jnp.sum(jnp.where(lanes == me_expert, totals, 0.0), axis=1, keepdims=True)
    beta = own_load / (own_load + mean_load)
    beta_out[...] = jnp.broadcast_to(beta, beta_out.shape)

    for layer in range(LAYERS):
        def land(b, _):
            g_copy(layer, b, 0).wait_recv()
            return 0
        lax.fori_loop(0, BLOCKS, land, 0)
    out_copy = pltpu.make_async_copy(gbuf, grad, out_sem)
    out_copy.start()

    def sent(layer):
        def body(j, _):
            y_copy(layer, j).wait_send()
            y_pass(layer, j).wait_send()
            z_copy(layer, j).wait_send()
            z_pass(layer, j).wait_send()
            return 0
        lax.fori_loop(0, 4, body, 0)

        def body_g(b, _):
            g_copy(layer, b, 0).wait_send()
            return 0
        lax.fori_loop(0, BLOCKS, body_g, 0)

    sent(0)
    sent(1)
    each(lambda b: x_copy(1, b), 0, BLOCKS, "wait_send")
    a_copy.wait_send()
    each(c_copy, 1, 8, "wait_send")
    each(d_copy, 1, 32, "wait_send")

    each(q_copy, 1, 32, "wait_recv")
    total = jnp.sum(q_own[...] + jnp.sum(q_got[...], axis=0), axis=1, keepdims=True)
    root_mean = jnp.sqrt(total / float(rows * 2 * half_cols))
    factor = step_size * (own_load / mean_load) * clip_level / jnp.maximum(root_mean, clip_level)
    factor_out[...] = jnp.broadcast_to(factor, factor_out.shape)
    each(q_copy, 1, 32, "wait_send")
    out_copy.wait()


def on_device(activations, out_grads, weights, shadow, counts):
    acts, og, counts = activations[:, 0], out_grads[:, 0], counts
    tokens, rows = acts.shape[1:]
    ff = og.shape[2]
    width = ff // 2 // BLOCKS
    unit = rows // 2 // NZ
    f32 = jnp.float32
    dma = pltpu.SemaphoreType.DMA
    vmem = pl.BlockSpec(memory_space=pltpu.VMEM)
    hbm = pl.BlockSpec(memory_space=pl.ANY)
    half = rows // 2
    grad, factor, beta = pl.pallas_call(
        kernel,
        out_shape=(
            jax.ShapeDtypeStruct((LAYERS, unit // 2, ff), f32),
            jax.ShapeDtypeStruct((LAYERS, 128), f32),
            jax.ShapeDtypeStruct((LAYERS, 128), f32),
        ),
        in_specs=[vmem, hbm, vmem],
        out_specs=(hbm, vmem, vmem),
        scratch_shapes=[
            pltpu.VMEM((LAYERS, BLOCKS, rows, width), f32),
            pltpu.VMEM((24, NZ - 1, unit, width), f32),
            pltpu.VMEM((LAYERS, BLOCKS - ZF, half, width), f32),
            pltpu.VMEM((LAYERS, BLOCKS - ZF, half, width), f32),
            pltpu.VMEM((LAYERS, ZF, unit, width), f32),
            pltpu.VMEM((LAYERS, ZF, unit, width), f32),
            pltpu.VMEM((LAYERS, BLOCKS, tokens, width), f32),
            pltpu.VMEM((BLOCKS, tokens, width), f32),
            pltpu.VMEM((LAYERS, BLOCKS, tokens, width), jnp.bfloat16),
            pltpu.VMEM((LAYERS, BLOCKS, tokens, width), jnp.bfloat16),
            pltpu.VMEM((LAYERS, tokens, rows), f32),
            pltpu.VMEM((LAYERS, tokens, rows), f32),
            pltpu.VMEM((rows, 2 * tokens), f32),
            pltpu.VMEM((LAYERS, rows, 2 * tokens), jnp.bfloat16),
            pltpu.VMEM((LAYERS, unit // 2, ff), f32),
            pltpu.VMEM((LAYERS, 128), f32),
            pltpu.VMEM((7, LAYERS, 128), f32),
            pltpu.VMEM((LAYERS, 128), f32),
            pltpu.VMEM((31, LAYERS, 128), f32),
            pltpu.VMEM((LAYERS, 128), f32),
            pltpu.VMEM((31, LAYERS, 128), f32),
            pltpu.VMEM((LAYERS, unit // 2, 128), f32),
            dma((LAYERS, 2, BLOCKS)),
            dma((BLOCKS,)),
            dma((LAYERS, BLOCKS)),
            dma((2,)),
            dma((24,)),
            dma((24, NZ - 1)),
            dma((4, LAYERS, BLOCKS - ZF)),
            dma((4, LAYERS, ZF)),
            dma((2, LAYERS, BLOCKS)),
            dma((2, 7)),
            dma((2, 31)),
            dma((2, 31)),
            dma,
        ],
        compiler_params=pltpu.CompilerParams(
            collective_id=0, has_side_effects=True, vmem_limit_bytes=62 * 1024 * 1024
        ),
    )(acts, og, counts)
    summed = grad[:, None]
    factor = factor[:, None, None, :1]
    beta = beta[:, None, None, :1]
    updated = weights - factor * summed
    return updated, shadow + beta * (updated - shadow)


def solution(mesh):
    split = Mesh(
        mesh.devices.reshape(mesh.shape["dp"], 4, 2, 2, 2),
        ("dp", "expert_0", "expert_1", "shard_0", "shard_1"),
    )
    return jax.shard_map(
        on_device,
        mesh=split,
        in_specs=(
            P(None, EXPERT, DP_SHARD, None),
            P(None, EXPERT, DP_SHARD, None),
            P(None, EXPERT, DP_SHARD, None),
            P(None, EXPERT, DP_SHARD, None),
            P(None, DP_EXPERT_SHARD, None),
        ),
        out_specs=(P(None, EXPERT, DP_SHARD, None), P(None, EXPERT, DP_SHARD, None)),
        check_vma=False,
    )
```

time: 423 us -> 154 us (0.36)
  waiting for transfers between devices: 311 us -> 0 us
  Pallas kernels: 0 us -> 149 us
  blocking collectives: 37.9 us -> 0 us
  starting transfers between devices: 21.2 us -> 0 us
  between operations: 20.7 us -> 0.67 us
  matrix products: 18.7 us -> 0 us
  other arithmetic: 8.65 us -> 2.64 us
    reduce_scatter x2 -> x0, waiting for transfers between devices: 303 us -> none  [on_device(): lax.psum_scatter(term(jnp.int32(0), lax.axis_size(DP_SHARD) * own_rows),...]
    pallas_call x0 -> x1, Pallas kernels: none -> 149 us  [on_device(): pl.pallas_call(kernel, out_shape=(jax.ShapeDtypeStruct((LAYERS, unit // 2...]
    psum x5 -> x0, blocking collectives: 37.9 us -> none  [by_axis(): value = lax.psum(value, axis)]
    all_to_all x2 -> x0, starting transfers between devices: 21.2 us -> none  [sent_to_all(): return lax.all_to_all(copies, axis, split_axis=0, concat_axis=0, tiled=True)]
    dot_general x2 -> x0, matrix products: 18.7 us -> none  [partial_rows(): lax.dot_general(inputs, cotangent, (((0,), (0,)), ((), ())), preferred_el...]
    all_to_all x2 -> x0, waiting for transfers between devices: 7.98 us -> none  [sent_to_all(): return lax.all_to_all(copies, axis, split_axis=0, concat_axis=0, tiled=True)]
    reduce_sum x6 -> x0, other arithmetic: 5.96 us -> none  [the longest x2 3.48 us: on_device(): squares = jnp.sum(summed * summed)]
  transfers between devices with their start and end apart: 4 -> 0, of which waited for: 3 -> 0; matrix products, arithmetic and copies ran while one was open for 4% -> 0% of each run, Pallas kernels for 0% -> 0%
where the time goes in v1:
time: 154 us; the launch traced here: 153 us
  Pallas kernels  149 us (97%)
  other arithmetic  2.64 us (2%)
    pallas_call x1, Pallas kernels, on_device(): pl.pallas_call(kernel, out_shape=(jax.ShapeDtypeStruct((LAYERS, unit // 2...  149 us

profile of v1, /device:TPU:1, one launch (start us, length us, event | category | flops | bytes accessed | tf_op | source)
XLA Modules:
  0.0 153.4 jit_solution(3088915664621240012)
XLA Ops:
  0.6 0.0 copy-start
  0.6 0.0 copy-start.1
  0.7 149.3 %shard_map.68 = (f32[2,8,14336]{2,1,0:T(8,128)}, f32[2,128]{1,0:T(2,128)}, f32[2,128]{1,0:T(2,128)}) custom-call(bf16[2,128,256]{2,1,0:T(8,128)(2,1)} %bitcast.28, bf16[2,128,14336]{2,1,0:T(8,128)(2,1)} %bitcast.27, s32[2,1,8]{2,1,0:T(1,128)} %counts.1), custom_call_target="tpu_custom_call" | custom-call | tf_op jit(solution)/shard_map/pallas_call | solution.py:431
  149.9 0.8 slice_reduce_fusion
  150.7 0.0 copy-done
  150.7 0.0 copy-done.1
  150.8 2.6 %fusion = (f32[2,1,8,14336]{3,2,1,0:T(8,128)}, f32[2,1,8,14336]{3,2,1,0:T(8,128)}) fusion(f32[2,1,8,14336]{3,2,1,0:T(8,128)S(1)} %copy-done, f32[2]{0:T(128)S(1)} %get-tuple-element.14, f32[2,8,14336]{2,1,0:T(8,128)} %get-tuple-element.6, f32[2]{0:T(128)S(1)} %get-tuple-element.15, f32[2,1,8,14336]{3,2,1,0:T(8,128)S(1)} %copy-done.1), kind=kLoop, calls=%fused_computation.2 | loop fusion | flops 1146880 | bytes 4587536
Async XLA Ops:
  0.6 150.1 %copy-start = (f32[2,1,8,14336]{3,2,1,0:T(8,128)S(1)}, f32[2,1,8,14336]{3,2,1,0:T(8,128)}, u32[]{:S(2)}) copy-start(f32[2,1,8,14336]{3,2,1,0:T(8,128)} %param.8) | copy-start | bytes 2752516
  0.6 150.1 %copy-start.1 = (f32[2,1,8,14336]{3,2,1,0:T(8,128)S(1)}, f32[2,1,8,14336]{3,2,1,0:T(8,128)}, u32[]{:S(2)}) copy-start(f32[2,1,8,14336]{3,2,1,0:T(8,128)} %param.7) | copy-start | bytes 2752516

commit v2 on v1

--- a/solution.py
+++ b/solution.py
@@ -119,9 +119,6 @@
         x_copy(0, b).start()
         return 0
 
-    x_copy(0, 0).start()
-    lax.fori_loop(1, BLOCKS, swap, 0)
-
     def c_copy(offset):
         return remote(c_own, c_got.at[offset - 1], c_sem.at[0, offset - 1], c_sem.at[1, offset - 1], expert_device(offset))
 
@@ -130,6 +127,10 @@
             getattr(copy(i), what)()
             return 0
         lax.fori_loop(low, high, body, 0)
+
+    x_copy(0, 0).start()
+    lax.fori_loop(1, BLOCKS, swap, 0)
+    each(c_copy, 1, 8, "start")
 
     a_copy.wait_recv()
     for layer in range(LAYERS):
@@ -147,54 +148,70 @@
         both = jnp.concatenate([own_half[layer, b], x_got[layer, b].astype(jnp.bfloat16)], axis=0)
         part[layer, b] = jnp.dot(a_t[layer], both, preferred_element_type=jnp.float32)
 
-    def stream(phase, slot):
-        if phase < 2:
-            return phase, slot // 2, lax.rem(slot, 2)
-        return slot // 4, ZF + lax.rem(slot, 4), 0
-
-    def sign_of(b):
-        return 1 - 2 * lax.rem(b, 2)
+    def sign_of(slot):
+        return 1 - 2 * lax.rem(slot, 2)
+
+    def block_of(k):
+        if isinstance(k, tuple):
+            layer, slot = k
+            return layer, slot // 4 * 4 + lax.rem(slot, 2), lax.rem(slot // 2, 2), layer * 8 + slot
+        return k // 4, lax.rem(k, 4) // 2 * 4 + 2 + lax.rem(k, 2), 0, 16 + k
+
+    def parity(k):
+        return sign_of(k[1] if isinstance(k, tuple) else k)
 
     def chunk(layer, b, half, index):
         return part.at[layer, b, pl.ds(pl.multiple_of(half * half_rows + index * unit, unit), unit), :]
 
-    def ring_copy(phase, slot, step):
-        layer, b, half = stream(phase, slot)
-        sign = sign_of(b)
-        k = phase * 8 + slot
+    def ring_copy(stream, step):
+        layer, b, half, k = block_of(stream)
+        sign = parity(stream)
         if step == 0:
             src = chunk(layer, b, half, lax.rem(z - sign + NZ, NZ))
         else:
             src = ring.at[k, step - 1]
         return remote(src, ring.at[k, step], ring_send.at[k], ring_recv.at[k, step], z_next(sign))
 
-    def ring_step(phase, slot, step):
-        layer, b, half = stream(phase, slot)
-        k = phase * 8 + slot
-        before = ring_copy(phase, slot, step - 1)
+    def ring_step(stream, step):
+        layer, b, half, k = block_of(stream)
+        before = ring_copy(stream, step - 1)
         before.wait_recv()
-        index = lax.rem(z - sign_of(b) * (1 + step) + 2 * NZ, NZ)
+        index = lax.rem(z - parity(stream) * (1 + step) + 2 * NZ, NZ)
         ring[k, step - 1] = ring[k, step - 1] + chunk(layer, b, half, index)[...]
         before.wait_send()
-        ring_copy(phase, slot, step).start()
-
-    def ring_last(phase, slot):
-        layer, b, half = stream(phase, slot)
-        k = phase * 8 + slot
-        before = ring_copy(phase, slot, NZ - 2)
+        ring_copy(stream, step).start()
+
+    def ring_last(stream):
+        layer, b, half, k = block_of(stream)
+        before = ring_copy(stream, NZ - 2)
         before.wait_recv()
         before.wait_send()
         return ring[k, NZ - 2] + chunk(layer, b, half, z)[...]
 
-    def round_of(phase, step, low=0, high=8):
-        def body(slot, _):
-            ring_step(phase, slot, step)
+    def loop(low, high, act):
+        def body(i, _):
+            act(i)
             return 0
         lax.fori_loop(low, high, body, 0)
 
+    def z_steps(layer, low, high, step):
+        loop(low, high, lambda slot: ring_step((layer, slot), step))
+
+    def y_steps(low, high, step):
+        loop(low, high, lambda slot: ring_step(slot, step))
+
+    def z_start(layer, low, high):
+        loop(low, high, lambda slot: ring_copy((layer, slot), 0).start())
+
+    def z_end(layer, low, high):
+        def act(slot):
+            ring[layer * 8 + slot, NZ - 2] = ring_last((layer, slot))
+        loop(low, high, act)
+
     def y_copy(layer, j):
+        b = j // 2 * 4 + 2 + lax.rem(j, 2)
         return remote(
-            part.at[layer, ZF + j, pl.ds(half_rows, half_rows), :], y_relay.at[layer, j],
+            part.at[layer, b, pl.ds(half_rows, half_rows), :], y_relay.at[layer, j],
             y_sem.at[0, layer, j], y_sem.at[1, layer, j], y_next(sign_of(j)),
         )
 
@@ -204,15 +221,23 @@
         )
 
     def y_forward(layer, low, high):
-        def body(j, _):
+        def act(j):
             y_copy(layer, j).wait_recv()
             y_pass(layer, j).start()
-            return 0
-        lax.fori_loop(low, high, body, 0)
+        loop(low, high, act)
+
+    def y_start(low, high):
+        def act(slot):
+            layer, b, _, _ = block_of(slot)
+            j = lax.rem(slot, 4)
+            y_pass(layer, j).wait_recv()
+            part[layer, b, 0:half_rows, :] = part[layer, b, 0:half_rows, :] + y_got[layer, j]
+            ring_copy(slot, 0).start()
+        loop(low, high, act)
 
     def z_copy(layer, j):
         return remote(
-            ring.at[layer * 8 + j * 2 + 1, NZ - 2], z_relay.at[layer, j],
+            ring.at[layer * 8 + j // 2 * 4 + 2 + lax.rem(j, 2), NZ - 2], z_relay.at[layer, j],
             z_sem.at[0, layer, j], z_sem.at[1, layer, j], y_next(sign_of(j)),
         )
 
@@ -222,11 +247,10 @@
         )
 
     def z_forward(layer):
-        def body(j, _):
+        def act(j):
             z_copy(layer, j).wait_recv()
             z_pass(layer, j).start()
-            return 0
-        lax.fori_loop(0, ZF, body, 0)
+        loop(0, ZF, act)
 
     def gcols(side, b):
         return pl.ds(pl.multiple_of(side * half_cols + b * width, 128), width)
@@ -246,130 +270,112 @@
             total = total + folded[:, i * 128 : (i + 1) * 128]
         q_acc[layer] = q_acc[layer] + total
 
-    def zf_end(layer):
-        def body(j, _):
-            slot = j * 2 + 1
-            ring[layer * 8 + slot, NZ - 2] = ring_last(layer, slot)
-            z_copy(layer, j).start()
-            slot = j * 2
-            ring[layer * 8 + slot, NZ - 2] = ring_last(layer, slot)
-            return 0
-        lax.fori_loop(0, ZF, body, 0)
-
-    def zf_finish(layer):
-        def body(j, _):
+    def z_finish(layer):
+        def act(j):
             z_pass(layer, j).wait_recv()
-            k = layer * 8 + j * 2
-            finish(layer, j, k, ring[k, NZ - 2] + z_got[layer, j])
-            return 0
-        lax.fori_loop(0, ZF, body, 0)
-
-    def zf_begin(layer):
-        def body(b, _):
-            multiply(layer, b)
-            return 0
-        lax.fori_loop(0, ZF, body, 0)
-
-    def zf_start(phase):
-        def body(slot, _):
-            ring_copy(phase, slot, 0).start()
-            return 0
-        lax.fori_loop(0, 8, body, 0)
-
-    def first(b, _):
-        multiply(0, b)
-        ring_copy(0, b * 2, 0).start()
-        ring_copy(0, b * 2 + 1, 0).start()
-        return 0
-
-    lax.fori_loop(0, ZF, first, 0)
-
-    def second(j, _):
-        multiply(0, ZF + j)
-        y_copy(0, j).start()
-        return 0
-
-    lax.fori_loop(0, BLOCKS - ZF, second, 0)
-    each(c_copy, 1, 8, "start")
-
-    def swap_again(b, _):
+            k = layer * 8 + j // 2 * 4 + lax.rem(j, 2)
+            finish(layer, j // 2 * 4 + lax.rem(j, 2), k, ring[k, NZ - 2] + z_got[layer, j])
+        loop(0, ZF, act)
+
+    def y_finish(low, high):
+        def act(slot):
+            layer, b, _, k = block_of(slot)
+            finish(layer, b, k, ring_last(slot))
+        loop(low, high, act)
+
+    def d_copy(offset):
+        return remote(d_own, d_got.at[offset - 1], d_sem.at[0, offset - 1], d_sem.at[1, offset - 1], group_device(offset))
+
+    def q_copy(offset):
+        return remote(q_own, q_got.at[offset - 1], q_sem.at[0, offset - 1], q_sem.at[1, offset - 1], group_device(offset))
+
+    for pair in range(2):
+        def first(odd):
+            multiply(0, pair * 4 + odd)
+            ring_copy((0, pair * 4 + odd), 0).start()
+            ring_copy((0, pair * 4 + 2 + odd), 0).start()
+
+        loop(0, 2, first)
+
+        def second(odd):
+            multiply(0, pair * 4 + 2 + odd)
+            y_copy(0, pair * 2 + odd).start()
+
+        loop(0, 2, second)
+
+    def swap_again(b):
         x_copy(0, b).wait_send()
         convert(1, b)
         x_copy(1, b).start()
-        return 0
-
-    lax.fori_loop(0, BLOCKS, swap_again, 0)
-    round_of(0, 1)
-
-    def more(b, _):
-        multiply(1, b)
-        return 0
-
-    lax.fori_loop(0, ZF, more, 0)
-    round_of(0, 2)
-    lax.fori_loop(ZF, BLOCKS, more, 0)
-    round_of(0, 3)
+
+    loop(0, BLOCKS, swap_again)
+    z_steps(0, 0, 8, 1)
+    loop(0, 2, lambda b: multiply(1, b))
+    z_start(1, 0, 2)
+    z_steps(0, 0, 8, 2)
+    z_steps(1, 0, 2, 1)
     y_forward(0, 0, 2)
-
+    loop(2, BLOCKS, lambda b: multiply(1, b))
+    z_steps(0, 0, 8, 3)
+    z_steps(1, 0, 2, 2)
+    z_steps(0, 0, 8, 4)
+    z_steps(1, 0, 2, 3)
+    y_forward(0, 2, 4)
+    each(lambda j: y_copy(1, j), 0, 4, "start")
     each(c_copy, 1, 8, "wait_recv")
     d_own[...] = c_own[...] + jnp.sum(c_got[...], axis=0)
-
-    def d_copy(offset):
-        return remote(d_own, d_got.at[offset - 1], d_sem.at[0, offset - 1], d_sem.at[1, offset - 1], group_device(offset))
-
     each(d_copy, 1, 32, "start")
-    round_of(0, 4)
-    round_of(0, 5)
-    y_forward(0, 2, 4)
-    each(lambda j: y_copy(1, j), 0, 4, "start")
-    round_of(0, 6)
-
-    zf_start(1)
-    zf_end(0)
-    round_of(1, 1)
-    round_of(1, 2)
-    round_of(1, 3)
-    round_of(1, 4)
+    z_steps(0, 0, 8, 5)
+    z_steps(1, 0, 2, 4)
+    z_steps(0, 0, 8, 6)
+    z_steps(1, 0, 2, 5)
+
+    z_start(1, 2, 8)
+    y_start(0, 2)
+    z_end(0, 0, 8)
+    z_steps(1, 0, 2, 6)
+    z_steps(1, 2, 8, 1)
+    y_steps(0, 2, 1)
+    z_end(1, 0, 2)
+    z_steps(1, 2, 8, 2)
+    y_steps(0, 2, 2)
     y_forward(1, 0, 2)
-    round_of(1, 5)
+    z_steps(1, 2, 8, 3)
+    y_steps(0, 2, 3)
+    z_steps(1, 2, 8, 4)
+    y_steps(0, 2, 4)
+    y_forward(1, 2, 4)
+    each(lambda j: z_copy(0, j), 0, 4, "start")
+    z_steps(1, 2, 8, 5)
+    y_steps(0, 2, 5)
+    z_steps(1, 2, 8, 6)
+    y_steps(0, 2, 6)
+
+    y_start(2, 6)
+    z_end(1, 2, 8)
+    each(lambda j: z_copy(1, j), 0, 4, "start")
+    y_finish(0, 2)
+    y_start(6, 8)
+    y_steps(2, 8, 1)
+    y_steps(2, 8, 2)
     z_forward(0)
-    round_of(1, 6)
-    y_forward(1, 2, 4)
-
-    def yf_start(slot, _):
-        layer, b, half = stream(2, slot)
-        y_pass(layer, b - ZF).wait_recv()
-        part[layer, b, 0:half_rows, :] = part[layer, b, 0:half_rows, :] + y_got[layer, b - ZF]
-        ring_copy(2, slot, 0).start()
-        return 0
-
-    lax.fori_loop(0, 4, yf_start, 0)
-    zf_end(1)
-    lax.fori_loop(4, 6, yf_start, 0)
-    zf_finish(0)
-    round_of(2, 1, 0, 6)
     z_forward(1)
-    lax.fori_loop(6, 8, yf_start, 0)
-    for step in range(2, 7):
-        round_of(2, step, 0, 6)
-        round_of(2, step - 1, 6, 8)
-    zf_finish(1)
-
-    def yf_end(slot, _):
-        layer, b, half = stream(2, slot)
-        finish(layer, b, 16 + slot, ring_last(2, slot))
-        return 0
-
-    lax.fori_loop(0, 6, yf_end, 0)
-    round_of(2, 6, 6, 8)
-    lax.fori_loop(6, 8, yf_end, 0)
+    y_steps(2, 8, 3)
+    y_steps(2, 8, 4)
+    z_finish(0)
+    y_steps(2, 8, 5)
+    z_finish(1)
+    y_steps(2, 8, 6)
+    y_finish(2, 8)
 
     q_own[...] = jnp.sum(q_acc[...], axis=1)
 
-    def q_copy(offset):
-        return remote(q_own, q_got.at[offset - 1], q_sem.at[0, offset - 1], q_sem.at[1, offset - 1], group_device(offset))
-
-    each(q_copy, 1, 32, "start")
+    def far_first(i):
+        m = i // 4
+        q_copy((4 + m // 2 - lax.rem(m, 2) * (2 * (m // 2) + 1)) * 4 + lax.rem(i, 4)).start()
+
+    loop(0, 28, far_first)
+    each(q_copy, 1, 4, "start")
 
     each(d_copy, 1, 32, "wait_recv")
     totals = d_own[...] + jnp.sum(d_got[...], axis=0)
@@ -377,43 +383,35 @@
     mean_load = jnp.sum(totals, axis=1, keepdims=True) / 8.0
     own_load = jnp.sum(jnp.where(lanes == me_expert, totals, 0.0), axis=1, keepdims=True)
     beta = own_load / (own_load + mean_load)
-    beta_out[...] = jnp.broadcast_to(beta, beta_out.shape)
 
     for layer in range(LAYERS):
-        def land(b, _):
-            g_copy(layer, b, 0).wait_recv()
-            return 0
-        lax.fori_loop(0, BLOCKS, land, 0)
+        loop(0, BLOCKS, lambda b: g_copy(layer, b, 0).wait_recv())
     out_copy = pltpu.make_async_copy(gbuf, grad, out_sem)
     out_copy.start()
 
-    def sent(layer):
-        def body(j, _):
+    for layer in range(LAYERS):
+        def sent(j):
             y_copy(layer, j).wait_send()
             y_pass(layer, j).wait_send()
             z_copy(layer, j).wait_send()
             z_pass(layer, j).wait_send()
-            return 0
-        lax.fori_loop(0, 4, body, 0)
-
-        def body_g(b, _):
-            g_copy(layer, b, 0).wait_send()
-            return 0
-        lax.fori_loop(0, BLOCKS, body_g, 0)
-
-    sent(0)
-    sent(1)
+
+        loop(0, 4, sent)
+        loop(0, BLOCKS, lambda b: g_copy(layer, b, 0).wait_send())
+
     each(lambda b: x_copy(1, b), 0, BLOCKS, "wait_send")
     a_copy.wait_send()
     each(c_copy, 1, 8, "wait_send")
     each(d_copy, 1, 32, "wait_send")
+    each(q_copy, 1, 32, "wait_send")
 
     each(q_copy, 1, 32, "wait_recv")
     total = jnp.sum(q_own[...] + jnp.sum(q_got[...], axis=0), axis=1, keepdims=True)
     root_mean = jnp.sqrt(total / float(rows * 2 * half_cols))
     factor = step_size * (own_load / mean_load) * clip_level / jnp.maximum(root_mean, clip_level)
-    factor_out[...] = jnp.broadcast_to(factor, factor_out.shape)
-    each(q_copy, 1, 32, "wait_send")
+    for layer in range(LAYERS):
+        factor_out[layer] = factor[layer, 0]
+        beta_out[layer] = beta[layer, 0]
     out_copy.wait()
 
 
@@ -426,17 +424,18 @@
     f32 = jnp.float32
     dma = pltpu.SemaphoreType.DMA
     vmem = pl.BlockSpec(memory_space=pltpu.VMEM)
+    smem = pl.BlockSpec(memory_space=pltpu.SMEM)
     hbm = pl.BlockSpec(memory_space=pl.ANY)
     half = rows // 2
     grad, factor, beta = pl.pallas_call(
         kernel,
         out_shape=(
             jax.ShapeDtypeStruct((LAYERS, unit // 2, ff), f32),
-            jax.ShapeDtypeStruct((LAYERS, 128), f32),
-            jax.ShapeDtypeStruct((LAYERS, 128), f32),
+            jax.ShapeDtypeStruct((LAYERS,), f32),
+            jax.ShapeDtypeStruct((LAYERS,), f32),
         ),
         in_specs=[vmem, hbm, vmem],
-        out_specs=(hbm, vmem, vmem),
+        out_specs=(hbm, smem, smem),
         scratch_shapes=[
             pltpu.VMEM((LAYERS, BLOCKS, rows, width), f32),
             pltpu.VMEM((24, NZ - 1, unit, width), f32),
@@ -479,8 +478,8 @@
         ),
     )(acts, og, counts)
     summed = grad[:, None]
-    factor = factor[:, None, None, :1]
-    beta = beta[:, None, None, :1]
+    factor = factor[:, None, None, None]
+    beta = beta[:, None, None, None]
     updated = weights - factor * summed
     return updated, shadow + beta * (updated - shadow)
 

time: 154 us -> 139 us (0.903)
  Pallas kernels: 149 us -> 136 us
    pallas_call x1, Pallas kernels: 149 us -> 136 us  [on_device(): pl.pallas_call(kernel, out_shape=(jax.ShapeDtypeStruct((LAYERS, unit // 2...]
where the time goes in v2:
time: 139 us
  Pallas kernels  136 us (98%)
  other arithmetic  2.65 us (2%)
    pallas_call x1, Pallas kernels, on_device(): pl.pallas_call(kernel, out_shape=(jax.ShapeDtypeStruct((LAYERS, unit // 2...  136 us

profile of v2, /device:TPU:1, one launch (start us, length us, event | category | flops | bytes accessed | tf_op | source)
XLA Modules:
  0.0 139.0 jit_solution(1280563457206407980)
XLA Ops:
  0.6 0.0 copy-start
  0.6 0.0 copy-start.1
  0.7 135.6 %shard_map.68 = (f32[2,8,14336]{2,1,0:T(8,128)}, f32[2]{0:T(128)}, f32[2]{0:T(128)}) custom-call(bf16[2,128,256]{2,1,0:T(8,128)(2,1)} %bitcast.28, bf16[2,128,14336]{2,1,0:T(8,128)(2,1)} %bitcast.27, s32[2,1,8]{2,1,0:T(1,128)} %counts.1), custom_call_target="tpu_custom_call" | custom-call | tf_op jit(solution)/shard_map/pallas_call | solution.py:430
  136.3 0.0 copy-done
  136.3 0.0 copy-done.1
  136.3 2.6 %fusion = (f32[2,1,8,14336]{3,2,1,0:T(8,128)}, f32[2,1,8,14336]{3,2,1,0:T(8,128)}) fusion(f32[2,1,8,14336]{3,2,1,0:T(8,128)S(1)} %copy-done, f32[2]{0:T(128)} %get-tuple-element.7, f32[2,8,14336]{2,1,0:T(8,128)} %get-tuple-element.6, f32[2]{0:T(128)} %get-tuple-element.5, f32[2,1,8,14336]{3,2,1,0:T(8,128)S(1)} %copy-done.1), kind=kLoop, calls=%fused_computation.2 | loop fusion | flops 1146880 | bytes 4587536
Async XLA Ops:
  0.6 135.7 %copy-start = (f32[2,1,8,14336]{3,2,1,0:T(8,128)S(1)}, f32[2,1,8,14336]{3,2,1,0:T(8,128)}, u32[]{:S(2)}) copy-start(f32[2,1,8,14336]{3,2,1,0:T(8,128)} %param.8) | copy-start | bytes 2752516
  0.6 135.7 %copy-start.1 = (f32[2,1,8,14336]{3,2,1,0:T(8,128)S(1)}, f32[2,1,8,14336]{3,2,1,0:T(8,128)}, u32[]{:S(2)}) copy-start(f32[2,1,8,14336]{3,2,1,0:T(8,128)} %param.7) | copy-start | bytes 2752516

commit v3 on v0

v3 whole, which is shorter than its diff:
```python
import jax
import jax.numpy as jnp
from jax import lax
from jax.experimental import pallas as pl
from jax.experimental.pallas import tpu as pltpu
from jax.sharding import Mesh
from jax.sharding import PartitionSpec as P

MESH = pl.DeviceIdType.MESH
LAYERS = 2
EXPERT = ("expert_0", "expert_1")
DP_EXPERT_SHARD = ("dp", "expert_0", "expert_1", "shard_0", "shard_1")
DP_SHARD = ("dp", "shard_0", "shard_1")

step_size = 0.5
clip_level = 1.0

NZ = 8
BLOCKS = 4
Z, Y = 0, 1


def kernel(
    acts, og, counts, grad, factor_out, beta_out,
    part_z, part_y, ring_z, ring_y, y_got, y_relay, z_got, z_relay, x_got_z, x_got_y, x_out_z, x_out_y,
    own_half, other_half, a_out, a_got, a_rows, a_t, gbuf, c_own, c_got, d_own, d_got, q_own, q_got, q_acc,
    og_sem, x_send, x_recv, x_recv_late, a_sem, ring_send, ring_recv,
    y_send, y_mid, y_end, y_units, z_send, z_mid, z_end_sem, g_sem, c_sem, d_sem, q_sem, out_sem,
):
    z = lax.axis_index("dp")
    x = lax.axis_index("expert_0")
    y_lo = lax.axis_index("expert_1")
    y_hi = lax.axis_index("shard_0")
    core = lax.axis_index("shard_1")
    y = y_hi * 2 + y_lo
    tokens = acts.shape[1]
    rows = acts.shape[2]
    half_rows = rows // 2
    unit = half_rows // NZ
    own_rows = unit // 2
    part = (part_z, part_y)
    ring = (ring_z, ring_y)
    x_got = (x_got_z, x_got_y)
    x_out = (x_out_z, x_out_y)
    width = (part_z.shape[-1], part_y.shape[-1])
    first_col = (0, BLOCKS * width[Z])
    half_cols = BLOCKS * (width[Z] + width[Y])

    def at(z=z, x=x, y_lo=y_lo, y_hi=y_hi, core=core):
        return (z, x, y_lo, y_hi, core)

    def z_next(sign):
        return at(z=lax.rem(z + sign + NZ, NZ))

    def y_next(sign):
        to = lax.rem(y + sign + 4, 4)
        return at(y_lo=lax.rem(to, 2), y_hi=to // 2)

    mate = at(core=1 - core)
    me_group = z * 4 + y_hi * 2 + core
    me_expert = x * 2 + y_lo

    def group_device(offset):
        to = lax.rem(me_group + offset, 32)
        return at(z=to // 4, y_hi=lax.rem(to // 2, 2), core=lax.rem(to, 2))

    def expert_device(offset):
        to = lax.rem(me_expert + offset, 8)
        return at(x=to // 2, y_lo=lax.rem(to, 2))

    def remote(src, dst, send, recv, device):
        return pltpu.make_async_remote_copy(
            src_ref=src, dst_ref=dst, send_sem=send, recv_sem=recv, device_id=device, device_id_type=MESH
        )

    def loop(low, high, act):
        def body(i, _):
            act(i)
            return 0
        lax.fori_loop(low, high, body, 0)

    def og_copy(layer, which, kind):
        first = core if which == 0 else 1 - core
        to = own_half if which == 0 else other_half
        size = BLOCKS * width[kind]
        cols = pl.ds(pl.multiple_of(first * half_cols + first_col[kind], 128), size)
        return pltpu.make_async_copy(
            og.at[layer, :, cols], to.at[layer, :, first_col[kind] : first_col[kind] + size], og_sem.at[layer, which, kind]
        )

    for layer in range(LAYERS):
        for which, kind in ((1, Y), (0, Y), (1, Z), (0, Z)):
            og_copy(layer, which, kind).start()

    barrier = pltpu.get_barrier_semaphore()

    def greet(device):
        pl.semaphore_signal(barrier, inc=1, device_id=device, device_id_type=MESH)

    loop(1, 32, lambda offset: greet(group_device(offset)))
    loop(1, 8, lambda offset: greet(expert_device(offset)))
    greet(at(y_lo=1 - y_lo, y_hi=1 - y_hi))

    def cols_of(kind, j):
        return pl.ds(pl.multiple_of(first_col[kind] + j * width[kind], 128), width[kind])

    def convert(layer, kind, j):
        x_out[kind][j] = other_half[layer, :, cols_of(kind, j)].astype(jnp.float32)

    def x_copy(layer, kind, j):
        sem = x_recv.at[kind, j] if layer == 0 else x_recv_late.at[kind]
        return remote(x_out[kind].at[j], x_got[kind].at[layer, j], x_send.at[kind], sem, mate)

    def x_all(layer, kind):
        return remote(x_out[kind], x_got[kind].at[layer], x_send.at[kind], x_recv_late.at[kind], mate)

    a_out[...] = acts[...].astype(jnp.float32)
    c_own[...] = jnp.zeros_like(c_own)
    c_own[:, 0:8] = counts[:, 0, :].astype(jnp.float32)
    q_acc[...] = jnp.zeros_like(q_acc)
    og_copy(0, 1, Y).wait()
    loop(0, 2, lambda j: convert(0, Y, j))
    pl.semaphore_wait(barrier, 39)

    a_copy = remote(a_out, a_got, a_sem.at[0], a_sem.at[1], mate)
    a_copy.start()

    def swap(layer, kind, low, high):
        def act(j):
            convert(layer, kind, j)
            x_copy(layer, kind, j).start()
        loop(low, high, act)

    loop(0, 2, lambda j: x_copy(0, Y, j).start())
    og_copy(0, 1, Z).wait()
    swap(0, Z, 0, 4)
    swap(0, Y, 2, 4)

    def c_copy(offset):
        return remote(c_own, c_got.at[offset - 1], c_sem.at[0], c_sem.at[1], expert_device(offset))

    loop(1, 8, lambda offset: c_copy(offset).start())

    a_copy.wait_recv()
    for layer in range(LAYERS):
        a_rows[:, 0:tokens] = a_out[layer].T
        a_rows[:, tokens : 2 * tokens] = a_got[layer].T
        for half in range(2):
            side = y_hi if half == 0 else 1 - y_hi
            for zz in range(NZ):
                piece = a_rows[pl.ds(pl.multiple_of(zz * 2 * unit + side * unit, unit), unit), :]
                a_t[layer, half * half_rows + zz * unit : half * half_rows + (zz + 1) * unit, :] = piece.astype(jnp.bfloat16)

    def multiply(layer, kind, j):
        if layer == 0:
            x_copy(layer, kind, j).wait_recv()
        theirs = x_got[kind][layer, j].astype(jnp.bfloat16)
        both = jnp.concatenate([own_half[layer, :, cols_of(kind, j)], theirs], axis=0)
        part[kind][layer, j] = jnp.dot(a_t[layer], both, preferred_element_type=jnp.float32)

    def stream(kind, layer, slot):
        if kind == Z:
            return slot // 2, lax.rem(slot, 2), layer * 8 + slot, layer * 8 + slot
        return slot, 0, layer * 4 + slot, layer * 4 + slot

    def sign_of(slot):
        return 1 - 2 * lax.rem(slot, 2)

    def chunk(kind, layer, j, half, away):
        index = lax.rem(z + away + NZ, NZ)
        return part[kind].at[layer, j, pl.ds(pl.multiple_of(half * half_rows + index * unit, unit), unit), :]

    def long_copy(kind, layer, slot, step):
        j, half, k, sem = stream(kind, layer, slot)
        sign = sign_of(slot)
        src = chunk(kind, layer, j, half, sign * 4) if step == 0 else ring[kind].at[k, step - 1]
        return remote(src, ring[kind].at[k, step], ring_send.at[sem], ring_recv.at[sem, step % 2], z_next(sign))

    def short_copy(kind, layer, slot, step):
        j, half, k, sem = stream(kind, layer, slot)
        sign = sign_of(slot)
        src = chunk(kind, layer, j, half, sign * -3) if step == 0 else ring[kind].at[k, 4 + step - 1]
        return remote(src, ring[kind].at[k, 4 + step], ring_send.at[sem], ring_recv.at[sem, step % 2], z_next(-sign))

    def both_of(kind, layer, slot, step):
        _, _, k, sem = stream(kind, layer, slot)
        two = ring[kind].at[k, 0:2]
        return remote(two, two, ring_send.at[sem], ring_recv.at[sem, step % 2], z_next(1))

    def chain_start(kind, layer, slot):
        long_copy(kind, layer, slot, 0).start()
        short_copy(kind, layer, slot, 0).start()

    def chain_step(kind, layer, slot, step):
        j, half, k, _ = stream(kind, layer, slot)
        sign = sign_of(slot)
        before = both_of(kind, layer, slot, step - 1)
        before.wait_recv()
        ring[kind][k, step - 1] = ring[kind][k, step - 1] + chunk(kind, layer, j, half, sign * (4 - step))[...]
        if step < 3:
            ring[kind][k, 3 + step] = ring[kind][k, 3 + step] + chunk(kind, layer, j, half, sign * (step - 3))[...]
        before.wait_send()
        long_copy(kind, layer, slot, step).start()
        if step < 3:
            short_copy(kind, layer, slot, step).start()

    def chain_last(kind, layer, slot):
        j, half, k, _ = stream(kind, layer, slot)
        before = long_copy(kind, layer, slot, 3)
        before.wait_recv()
        before.wait_send()
        return k, ring[kind][k, 3] + chunk(kind, layer, j, half, 0)[...]

    def steps(kind, layer, low, high, step):
        loop(low, high, lambda slot: chain_step(kind, layer, slot, step))

    def starts(kind, layer, low, high):
        loop(low, high, lambda slot: chain_start(kind, layer, slot))

    def z_last(layer):
        def act(slot):
            k, value = chain_last(Z, layer, slot)
            ring_z[k, 3] = value + ring_z[k, 6]
        loop(0, 8, act)

    def y_copy(layer, j):
        return remote(
            part_y.at[layer, j, pl.ds(half_rows, half_rows), :], y_relay.at[layer, j],
            y_send.at[0], y_mid.at[layer, j // 2], y_next(sign_of(j)),
        )

    def y_pass(layer, j):
        return remote(y_relay.at[layer, j], y_got.at[layer, j], y_send.at[1], y_end.at[layer, j // 2], y_next(sign_of(j)))

    def pair(layer, p, sems):
        two = y_relay.at[layer, 2 * p : 2 * p + 2]
        return remote(two, two, y_send.at[1], sems.at[layer, p], mate)

    def y_forward(layer, p):
        pair(layer, p, y_mid).wait_recv()
        loop(2 * p, 2 * p + 2, lambda j: y_pass(layer, j).start())

    groups = ((4, -3), (3, -2), (2, -1), (1,), (0,))

    def unit_rows(away):
        return pl.ds(pl.multiple_of(lax.rem(z + away + NZ, NZ) * unit, unit), unit)

    def y_forward_units(layer, p):
        pair(layer, p, y_mid).wait_recv()
        for g, aways in enumerate(groups):
            for away in aways:
                def act(j):
                    sign = sign_of(j)
                    at_rows = unit_rows(sign * away)
                    remote(
                        y_relay.at[layer, j, at_rows, :], y_got.at[layer, j, at_rows, :],
                        y_send.at[1], y_units.at[g], y_next(sign),
                    ).start()
                loop(2 * p, 2 * p + 2, act)

    def y_units_add(layer, p, g):
        four = y_got.at[layer, 2 * p : 2 * p + 2, 0 : unit * len(groups[g]), :]
        remote(four, four, y_send.at[1], y_units.at[g], mate).wait_recv()
        for away in groups[g]:
            def act(j):
                at_rows = unit_rows(sign_of(j) * away)
                part_y[layer, j, at_rows, :] = part_y[layer, j, at_rows, :] + y_got[layer, j, at_rows, :]
            loop(2 * p, 2 * p + 2, act)

    def y_begin(layer, p):
        pair(layer, p, y_end).wait_recv()

        def act(j):
            part_y[layer, j, 0:half_rows, :] = part_y[layer, j, 0:half_rows, :] + y_got[layer, j]
            chain_start(Y, layer, j)
        loop(2 * p, 2 * p + 2, act)

    def z_copy(layer, j):
        return remote(
            ring_z.at[layer * 8 + j * 2 + 1, 3], z_relay.at[layer, j], z_send.at[0], z_mid.at[layer], y_next(sign_of(j))
        )

    def z_pass(layer, j):
        return remote(z_relay.at[layer, j], z_got.at[layer, j], z_send.at[1], z_end_sem.at[layer], y_next(sign_of(j)))

    def z_all(layer, sems):
        return remote(z_relay.at[layer], z_got.at[layer], z_send.at[1], sems.at[layer], mate)

    def z_forward(layer):
        z_all(layer, z_mid).wait_recv()
        loop(0, BLOCKS, lambda j: z_pass(layer, j).start())

    def gcols(side, kind, j):
        return pl.ds(pl.multiple_of(side * half_cols + first_col[kind] + j * width[kind], 128), width[kind])

    def finish(kind, layer, j, k, value):
        ring[kind][k, 3] = value
        src = ring[kind].at[k, 3, pl.ds(pl.multiple_of((1 - core) * own_rows, own_rows), own_rows), :]
        remote(src, gbuf.at[layer, :, gcols(core, kind, j)], g_sem.at[0], g_sem.at[1], mate).start()
        mine = ring[kind][k, 3, pl.ds(pl.multiple_of(core * own_rows, own_rows), own_rows), :]
        gbuf[layer, :, gcols(core, kind, j)] = mine
        squares = value * value
        folded = squares[0:own_rows] + squares[own_rows : 2 * own_rows]
        total = folded[:, 0:128]
        for i in range(1, width[kind] // 128):
            total = total + folded[:, i * 128 : (i + 1) * 128]
        q_acc[layer] = q_acc[layer] + total

    def z_finish(layer):
        z_all(layer, z_end_sem).wait_recv()

        def act(j):
            k = layer * 8 + j * 2
            finish(Z, layer, j, k, ring_z[k, 3] + z_got[layer, j])
        loop(0, BLOCKS, act)

    def y_finish(layer, low, high):
        def act(j):
            k, value = chain_last(Y, layer, j)
            finish(Y, layer, j, k, value + ring_y[k, 6])
        loop(low, high, act)

    def d_copy(offset):
        return remote(d_own, d_got.at[offset - 1], d_sem.at[0], d_sem.at[1], group_device(offset))

    def q_copy(offset):
        return remote(q_own, q_got.at[offset - 1], q_sem.at[0], q_sem.at[1], group_device(offset))

    def all_of(got, sems):
        return remote(got, got, sems.at[0], sems.at[1], mate)

    def to_y(j):
        multiply(0, Y, j)
        y_copy(0, j).start()

    def to_z(j):
        multiply(0, Z, j)
        chain_start(Z, 0, 2 * j)
        chain_start(Z, 0, 2 * j + 1)

    og_copy(0, 0, Y).wait()
    loop(0, 2, to_y)
    og_copy(0, 0, Z).wait()
    loop(0, 4, to_z)
    loop(2, 4, to_y)

    for kind in (Z, Y):
        x_all(0, kind).wait_send()
        og_copy(1, 1, kind).wait()
        swap(1, kind, 0, 4)
    og_copy(1, 0, Z).wait()
    og_copy(1, 0, Y).wait()

    steps(Z, 0, 0, 8, 1)
    x_all(1, Z).wait_recv()
    loop(0, 4, lambda j: multiply(1, Z, j))
    steps(Z, 0, 0, 8, 2)
    y_forward(0, 0)
    x_all(1, Y).wait_recv()
    loop(0, 4, lambda j: multiply(1, Y, j))
    steps(Z, 0, 0, 8, 3)
    starts(Z, 1, 0, 8)
    y_forward(0, 1)
    loop(0, 4, lambda j: y_copy(1, j).start())
    z_last(0)
    all_of(c_got, c_sem).wait_recv()
    d_own[...] = c_own[...] + jnp.sum(c_got[...], axis=0)
    loop(1, 32, lambda offset: d_copy(offset).start())

    steps(Z, 1, 0, 8, 1)
    steps(Z, 1, 0, 8, 2)
    steps(Z, 1, 0, 8, 3)
    y_begin(0, 0)
    y_begin(0, 1)
    z_last(1)
    y_forward(1, 0)
    steps(Y, 0, 0, 4, 1)
    steps(Y, 0, 0, 4, 2)
    y_forward_units(1, 1)
    for layer in range(LAYERS):
        loop(0, BLOCKS, lambda j: z_copy(layer, j).start())
    steps(Y, 0, 0, 4, 3)
    y_finish(0, 0, 4)

    y_begin(1, 0)
    y_units_add(1, 1, 0)
    starts(Y, 1, 2, 4)
    steps(Y, 1, 0, 2, 1)
    y_units_add(1, 1, 1)
    steps(Y, 1, 2, 4, 1)
    steps(Y, 1, 0, 2, 2)
    y_units_add(1, 1, 2)
    steps(Y, 1, 2, 4, 2)
    z_forward(0)
    z_forward(1)
    steps(Y, 1, 0, 2, 3)
    y_units_add(1, 1, 3)
    steps(Y, 1, 2, 4, 3)
    y_units_add(1, 1, 4)
    y_finish(1, 0, 2)
    z_finish(0)
    z_finish(1)
    y_finish(1, 2, 4)

    q_own[...] = jnp.sum(q_acc[...], axis=1)
    for away in (4, 3, 5, 2, 6, 1, 7):
        loop(away * 4, away * 4 + 4, lambda offset: q_copy(offset).start())
    loop(1, 4, lambda offset: q_copy(offset).start())

    all_of(d_got, d_sem).wait_recv()
    totals = d_own[...] + jnp.sum(d_got[...], axis=0)
    lanes = lax.broadcasted_iota(jnp.int32, totals.shape, 1)
    mean_load = jnp.sum(totals, axis=1, keepdims=True) / 8.0
    own_load = jnp.sum(jnp.where(lanes == me_expert, totals, 0.0), axis=1, keepdims=True)
    beta = own_load / (own_load + mean_load)

    landed = gbuf.at[:, :, 0:half_cols]
    all_g = remote(landed, landed, g_sem.at[0], g_sem.at[1], mate)
    all_g.wait_recv()
    out_copy = pltpu.make_async_copy(gbuf, grad, out_sem)
    out_copy.start()

    all_g.wait_send()
    for i in range(2):
        remote(y_relay, y_got, y_send.at[i], y_units.at[0], mate).wait_send()
        remote(z_relay, z_got, z_send.at[i], z_mid.at[0], mate).wait_send()
    for kind in (Z, Y):
        x_all(1, kind).wait_send()
    a_copy.wait_send()
    all_of(c_got, c_sem).wait_send()
    all_of(d_got, d_sem).wait_send()
    all_of(q_got, q_sem).wait_send()

    all_of(q_got, q_sem).wait_recv()
    total = jnp.sum(q_own[...] + jnp.sum(q_got[...], axis=0), axis=1, keepdims=True)
    root_mean = jnp.sqrt(total / float(rows * 2 * half_cols))
    factor = step_size * (own_load / mean_load) * clip_level / jnp.maximum(root_mean, clip_level)
    for layer in range(LAYERS):
        factor_out[layer] = factor[layer, 0]
        beta_out[layer] = beta[layer, 0]
    out_copy.wait()


def on_device(activations, out_grads, weights, shadow, counts):
    acts, og = activations[:, 0], out_grads[:, 0]
    tokens, rows = acts.shape[1:]
    ff = og.shape[2]
    unit = rows // 2 // NZ
    half = rows // 2
    tiles = ff // 2 // 128 // BLOCKS
    wide_z, wide_y = (tiles * 3 // 7) * 128, (tiles - tiles * 3 // 7) * 128
    f32, bf16 = jnp.float32, jnp.bfloat16
    dma = pltpu.SemaphoreType.DMA
    vmem = pl.BlockSpec(memory_space=pltpu.VMEM)
    smem = pl.BlockSpec(memory_space=pltpu.SMEM)
    hbm = pl.BlockSpec(memory_space=pl.ANY)
    grad, factor, beta = pl.pallas_call(
        kernel,
        out_shape=(
            jax.ShapeDtypeStruct((LAYERS, unit // 2, ff), f32),
            jax.ShapeDtypeStruct((LAYERS,), f32),
            jax.ShapeDtypeStruct((LAYERS,), f32),
        ),
        in_specs=[vmem, hbm, vmem],
        out_specs=(hbm, smem, smem),
        scratch_shapes=[
            pltpu.VMEM((LAYERS, BLOCKS, rows, wide_z), f32),
            pltpu.VMEM((LAYERS, BLOCKS, rows, wide_y), f32),
            pltpu.VMEM((LAYERS * 8, NZ - 1, unit, wide_z), f32),
            pltpu.VMEM((LAYERS * 4, NZ - 1, unit, wide_y), f32),
            pltpu.VMEM((LAYERS, BLOCKS, half, wide_y), f32),
            pltpu.VMEM((LAYERS, BLOCKS, half, wide_y), f32),
            pltpu.VMEM((LAYERS, BLOCKS, unit, wide_z), f32),
            pltpu.VMEM((LAYERS, BLOCKS, unit, wide_z), f32),
            pltpu.VMEM((LAYERS, BLOCKS, tokens, wide_z), f32),
            pltpu.VMEM((LAYERS, BLOCKS, tokens, wide_y), f32),
            pltpu.VMEM((BLOCKS, tokens, wide_z), f32),
            pltpu.VMEM((BLOCKS, tokens, wide_y), f32),
            pltpu.VMEM((LAYERS, tokens, ff // 2), bf16),
            pltpu.VMEM((LAYERS, tokens, ff // 2), bf16),
            pltpu.VMEM((LAYERS, tokens, rows), f32),
            pltpu.VMEM((LAYERS, tokens, rows), f32),
            pltpu.VMEM((rows, 2 * tokens), f32),
            pltpu.VMEM((LAYERS, rows, 2 * tokens), bf16),
            pltpu.VMEM((LAYERS, unit // 2, ff), f32),
            pltpu.VMEM((LAYERS, 128), f32),
            pltpu.VMEM((7, LAYERS, 128), f32),
            pltpu.VMEM((LAYERS, 128), f32),
            pltpu.VMEM((31, LAYERS, 128), f32),
            pltpu.VMEM((LAYERS, 128), f32),
            pltpu.VMEM((31, LAYERS, 128), f32),
            pltpu.VMEM((LAYERS, unit // 2, 128), f32),
            dma((LAYERS, 2, 2)),
            dma((2,)),
            dma((2, BLOCKS)),
            dma((2,)),
            dma((2,)),
            dma((16,)),
            dma((16, 2)),
            dma((2,)),
            dma((LAYERS, 2)),
            dma((LAYERS, 2)),
            dma((5,)),
            dma((2,)),
            dma((LAYERS,)),
            dma((LAYERS,)),
            dma((2,)),
            dma((2,)),
            dma((2,)),
            dma((2,)),
            dma,
        ],
        compiler_params=pltpu.CompilerParams(
            collective_id=0, has_side_effects=True, vmem_limit_bytes=62 * 1024 * 1024
        ),
    )(acts, og, counts)
    summed = grad[:, None]
    factor = factor[:, None, None, None]
    beta = beta[:, None, None, None]
    updated = weights - factor * summed
    return updated, shadow + beta * (updated - shadow)


def solution(mesh):
    split = Mesh(
        mesh.devices.reshape(mesh.shape["dp"], 4, 2, 2, 2),
        ("dp", "expert_0", "expert_1", "shard_0", "shard_1"),
    )
    return jax.shard_map(
        on_device,
        mesh=split,
        in_specs=(
            P(None, EXPERT, DP_SHARD, None),
            P(None, EXPERT, DP_SHARD, None),
            P(None, EXPERT, DP_SHARD, None),
            P(None, EXPERT, DP_SHARD, None),
            P(None, DP_EXPERT_SHARD, None),
        ),
        out_specs=(P(None, EXPERT, DP_SHARD, None), P(None, EXPERT, DP_SHARD, None)),
        check_vma=False,
    )
```

time: 423 us -> 134 us (0.32)
  waiting for transfers between devices: 311 us -> 0 us
  Pallas kernels: 0 us -> 130 us
  blocking collectives: 37.9 us -> 0 us
  starting transfers between devices: 21.2 us -> 0 us
  between operations: 20.7 us -> 0.67 us
  matrix products: 18.7 us -> 0 us
  other arithmetic: 8.65 us -> 2.65 us
    reduce_scatter x2 -> x0, waiting for transfers between devices: 303 us -> none  [on_device(): lax.psum_scatter(term(jnp.int32(0), lax.axis_size(DP_SHARD) * own_rows),...]
    pallas_call x0 -> x1, Pallas kernels: none -> 130 us  [on_device(): pl.pallas_call(kernel, out_shape=(jax.ShapeDtypeStruct((LAYERS, unit // 2...]
    psum x5 -> x0, blocking collectives: 37.9 us -> none  [by_axis(): value = lax.psum(value, axis)]
    all_to_all x2 -> x0, starting transfers between devices: 21.2 us -> none  [sent_to_all(): return lax.all_to_all(copies, axis, split_axis=0, concat_axis=0, tiled=True)]
    dot_general x2 -> x0, matrix products: 18.7 us -> none  [partial_rows(): lax.dot_general(inputs, cotangent, (((0,), (0,)), ((), ())), preferred_el...]
    all_to_all x2 -> x0, waiting for transfers between devices: 7.98 us -> none  [sent_to_all(): return lax.all_to_all(copies, axis, split_axis=0, concat_axis=0, tiled=True)]
    reduce_sum x6 -> x0, other arithmetic: 5.96 us -> none  [the longest x2 3.48 us: on_device(): squares = jnp.sum(summed * summed)]
  transfers between devices with their start and end apart: 4 -> 0, of which waited for: 3 -> 0; matrix products, arithmetic and copies ran while one was open for 4% -> 0% of each run, Pallas kernels for 0% -> 0%
where the time goes in v3:
time: 134 us; the launch traced here: 133 us
  Pallas kernels  130 us (97%)
  other arithmetic  2.65 us (2%)
    pallas_call x1, Pallas kernels, on_device(): pl.pallas_call(kernel, out_shape=(jax.ShapeDtypeStruct((LAYERS, unit // 2...  130 us

profile of v3, /device:TPU:1, one launch (start us, length us, event | category | flops | bytes accessed | tf_op | source)
XLA Modules:
  0.0 133.5 jit_solution(13376053303006252444)
XLA Ops:
  0.6 0.0 copy-start
  0.6 0.0 copy-start.1
  0.7 130.1 %shard_map.68 = (f32[2,8,14336]{2,1,0:T(8,128)}, f32[2]{0:T(128)}, f32[2]{0:T(128)}) custom-call(bf16[2,128,256]{2,1,0:T(8,128)(2,1)} %bitcast.28, bf16[2,128,14336]{2,1,0:T(8,128)(2,1)} %bitcast.27, s32[2,1,8]{2,1,0:T(1,128)} %counts.1), custom_call_target="tpu_custom_call" | custom-call | tf_op jit(solution)/shard_map/pallas_call | solution.py:457
  130.8 0.0 copy-done
  130.8 0.0 copy-done.1
  130.8 2.6 %fusion = (f32[2,1,8,14336]{3,2,1,0:T(8,128)}, f32[2,1,8,14336]{3,2,1,0:T(8,128)}) fusion(f32[2,1,8,14336]{3,2,1,0:T(8,128)S(1)} %copy-done, f32[2]{0:T(128)} %get-tuple-element.7, f32[2,8,14336]{2,1,0:T(8,128)} %get-tuple-element.6, f32[2]{0:T(128)} %get-tuple-element.5, f32[2,1,8,14336]{3,2,1,0:T(8,128)S(1)} %copy-done.1), kind=kLoop, calls=%fused_computation.2 | loop fusion | flops 1146880 | bytes 4587536
Async XLA Ops:
  0.6 130.2 %copy-start = (f32[2,1,8,14336]{3,2,1,0:T(8,128)S(1)}, f32[2,1,8,14336]{3,2,1,0:T(8,128)}, u32[]{:S(2)}) copy-start(f32[2,1,8,14336]{3,2,1,0:T(8,128)} %param.8) | copy-start | bytes 2752516
  0.6 130.2 %copy-start.1 = (f32[2,1,8,14336]{3,2,1,0:T(8,128)S(1)}, f32[2,1,8,14336]{3,2,1,0:T(8,128)}, u32[]{:S(2)}) copy-start(f32[2,1,8,14336]{3,2,1,0:T(8,128)} %param.7) | copy-start | bytes 2752516

commit v4 on v3

--- a/solution.py
+++ b/solution.py
@@ -21,11 +21,11 @@
 
 
 def kernel(
-    acts, og, counts, grad, factor_out, beta_out,
+    acts_in, og, counts_in, weights, shadow, new_weights, new_shadow,
     part_z, part_y, ring_z, ring_y, y_got, y_relay, z_got, z_relay, x_got_z, x_got_y, x_out_z, x_out_y,
-    own_half, other_half, a_out, a_got, a_rows, a_t, gbuf, c_own, c_got, d_own, d_got, q_own, q_got, q_acc,
-    og_sem, x_send, x_recv, x_recv_late, a_sem, ring_send, ring_recv,
-    y_send, y_mid, y_end, y_units, z_send, z_mid, z_end_sem, g_sem, c_sem, d_sem, q_sem, out_sem,
+    own_half, other_half, acts, counts, w_in, s_in, a_out, a_got, a_rows, a_t, gbuf, c_own, c_got, q_own, q_got, q_acc,
+    og_sem, in_sem, x_send, x_recv, x_recv_late, a_sem, ring_send, ring_recv,
+    y_send, y_mid, y_end, y_units, z_send, z_mid, z_end_sem, g_sem, c_sem, q_sem,
 ):
     z = lax.axis_index("dp")
     x = lax.axis_index("expert_0")
@@ -64,10 +64,6 @@
         to = lax.rem(me_group + offset, 32)
         return at(z=to // 4, y_hi=lax.rem(to // 2, 2), core=lax.rem(to, 2))
 
-    def expert_device(offset):
-        to = lax.rem(me_expert + offset, 8)
-        return at(x=to // 2, y_lo=lax.rem(to, 2))
-
     def remote(src, dst, send, recv, device):
         return pltpu.make_async_remote_copy(
             src_ref=src, dst_ref=dst, send_sem=send, recv_sem=recv, device_id=device, device_id_type=MESH
@@ -88,18 +84,25 @@
             og.at[layer, :, cols], to.at[layer, :, first_col[kind] : first_col[kind] + size], og_sem.at[layer, which, kind]
         )
 
+    in_copies = [
+        pltpu.make_async_copy(src, dst, in_sem.at[i])
+        for i, (src, dst) in enumerate(((acts_in, acts), (counts_in, counts), (weights, w_in), (shadow, s_in)))
+    ]
+
+    barrier = pltpu.get_barrier_semaphore()
+    near = (
+        mate, z_next(1), z_next(-1), y_next(1), y_next(-1), at(x=x + 1 - 2 * lax.rem(x, 2)), at(x=3 - x)
+    )
+    for device in near:
+        pl.semaphore_signal(barrier, inc=1, device_id=device, device_id_type=MESH)
+
+    in_copies[0].start()
+    in_copies[1].start()
     for layer in range(LAYERS):
         for which, kind in ((1, Y), (0, Y), (1, Z), (0, Z)):
             og_copy(layer, which, kind).start()
-
-    barrier = pltpu.get_barrier_semaphore()
-
-    def greet(device):
-        pl.semaphore_signal(barrier, inc=1, device_id=device, device_id_type=MESH)
-
-    loop(1, 32, lambda offset: greet(group_device(offset)))
-    loop(1, 8, lambda offset: greet(expert_device(offset)))
-    greet(at(y_lo=1 - y_lo, y_hi=1 - y_hi))
+    in_copies[2].start()
+    in_copies[3].start()
 
     def cols_of(kind, j):
         return pl.ds(pl.multiple_of(first_col[kind] + j * width[kind], 128), width[kind])
@@ -114,13 +117,15 @@
     def x_all(layer, kind):
         return remote(x_out[kind], x_got[kind].at[layer], x_send.at[kind], x_recv_late.at[kind], mate)
 
+    in_copies[0].wait()
     a_out[...] = acts[...].astype(jnp.float32)
-    c_own[...] = jnp.zeros_like(c_own)
-    c_own[:, 0:8] = counts[:, 0, :].astype(jnp.float32)
+    in_copies[1].wait()
+    c_own[0] = jnp.zeros_like(c_own[0])
+    c_own[0, :, 0:8] = counts[:, 0, :].astype(jnp.float32)
     q_acc[...] = jnp.zeros_like(q_acc)
     og_copy(0, 1, Y).wait()
     loop(0, 2, lambda j: convert(0, Y, j))
-    pl.semaphore_wait(barrier, 39)
+    pl.semaphore_wait(barrier, len(near))
 
     a_copy = remote(a_out, a_got, a_sem.at[0], a_sem.at[1], mate)
     a_copy.start()
@@ -136,10 +141,17 @@
     swap(0, Z, 0, 4)
     swap(0, Y, 2, 4)
 
-    def c_copy(offset):
-        return remote(c_own, c_got.at[offset - 1], c_sem.at[0], c_sem.at[1], expert_device(offset))
-
-    loop(1, 8, lambda offset: c_copy(offset).start())
+    c_copies = [
+        remote(c_own.at[i], c_got.at[i], c_sem.at[0, i], c_sem.at[1, i], device)
+        for i, device in enumerate((near[5], near[6], at(y_lo=1 - y_lo)))
+    ]
+    c_copies[0].start()
+
+    def c_next(i):
+        c_copies[i].wait_recv()
+        c_own[i + 1] = c_own[i] + c_got[i]
+        if i < 2:
+            c_copies[i + 1].start()
 
     a_copy.wait_recv()
     for layer in range(LAYERS):
@@ -320,9 +332,6 @@
             finish(Y, layer, j, k, value + ring_y[k, 6])
         loop(low, high, act)
 
-    def d_copy(offset):
-        return remote(d_own, d_got.at[offset - 1], d_sem.at[0], d_sem.at[1], group_device(offset))
-
     def q_copy(offset):
         return remote(q_own, q_got.at[offset - 1], q_sem.at[0], q_sem.at[1], group_device(offset))
 
@@ -363,12 +372,10 @@
     y_forward(0, 1)
     loop(0, 4, lambda j: y_copy(1, j).start())
     z_last(0)
-    all_of(c_got, c_sem).wait_recv()
-    d_own[...] = c_own[...] + jnp.sum(c_got[...], axis=0)
-    loop(1, 32, lambda offset: d_copy(offset).start())
-
+    c_next(0)
     steps(Z, 1, 0, 8, 1)
     steps(Z, 1, 0, 8, 2)
+    c_next(1)
     steps(Z, 1, 0, 8, 3)
     y_begin(0, 0)
     y_begin(0, 1)
@@ -380,9 +387,9 @@
     for layer in range(LAYERS):
         loop(0, BLOCKS, lambda j: z_copy(layer, j).start())
     steps(Y, 0, 0, 4, 3)
+    y_begin(1, 0)
     y_finish(0, 0, 4)
 
-    y_begin(1, 0)
     y_units_add(1, 1, 0)
     starts(Y, 1, 2, 4)
     steps(Y, 1, 0, 2, 1)
@@ -393,6 +400,7 @@
     steps(Y, 1, 2, 4, 2)
     z_forward(0)
     z_forward(1)
+    c_next(2)
     steps(Y, 1, 0, 2, 3)
     y_units_add(1, 1, 3)
     steps(Y, 1, 2, 4, 3)
@@ -402,23 +410,17 @@
     z_finish(1)
     y_finish(1, 2, 4)
 
-    q_own[...] = jnp.sum(q_acc[...], axis=1)
+    q_own[0:2] = jnp.sum(q_acc[...], axis=1)
+    q_own[2:4] = c_own[3]
     for away in (4, 3, 5, 2, 6, 1, 7):
         loop(away * 4, away * 4 + 4, lambda offset: q_copy(offset).start())
     loop(1, 4, lambda offset: q_copy(offset).start())
 
-    all_of(d_got, d_sem).wait_recv()
-    totals = d_own[...] + jnp.sum(d_got[...], axis=0)
-    lanes = lax.broadcasted_iota(jnp.int32, totals.shape, 1)
-    mean_load = jnp.sum(totals, axis=1, keepdims=True) / 8.0
-    own_load = jnp.sum(jnp.where(lanes == me_expert, totals, 0.0), axis=1, keepdims=True)
-    beta = own_load / (own_load + mean_load)
-
     landed = gbuf.at[:, :, 0:half_cols]
     all_g = remote(landed, landed, g_sem.at[0], g_sem.at[1], mate)
     all_g.wait_recv()
-    out_copy = pltpu.make_async_copy(gbuf, grad, out_sem)
-    out_copy.start()
+    in_copies[2].wait()
+    in_copies[3].wait()
 
     all_g.wait_send()
     for i in range(2):
@@ -427,18 +429,31 @@
     for kind in (Z, Y):
         x_all(1, kind).wait_send()
     a_copy.wait_send()
-    all_of(c_got, c_sem).wait_send()
-    all_of(d_got, d_sem).wait_send()
+    for copy in c_copies:
+        copy.wait_send()
     all_of(q_got, q_sem).wait_send()
 
     all_of(q_got, q_sem).wait_recv()
-    total = jnp.sum(q_own[...] + jnp.sum(q_got[...], axis=0), axis=1, keepdims=True)
-    root_mean = jnp.sqrt(total / float(rows * 2 * half_cols))
+    sums = q_own[...] + jnp.sum(q_got[...], axis=0)
+    root_mean = jnp.sqrt(jnp.sum(sums[0:2], axis=1, keepdims=True) / float(rows * 2 * half_cols))
+    totals = sums[2:4]
+    lanes = lax.broadcasted_iota(jnp.int32, totals.shape, 1)
+    mean_load = jnp.sum(totals, axis=1, keepdims=True) / 8.0
+    own_load = jnp.sum(jnp.where(lanes == me_expert, totals, 0.0), axis=1, keepdims=True)
     factor = step_size * (own_load / mean_load) * clip_level / jnp.maximum(root_mean, clip_level)
+    beta = own_load / (own_load + mean_load)
     for layer in range(LAYERS):
-        factor_out[layer] = factor[layer, 0]
-        beta_out[layer] = beta[layer, 0]
-    out_copy.wait()
+        this_factor = jnp.broadcast_to(factor[layer : layer + 1], (own_rows, 128))
+        this_beta = jnp.broadcast_to(beta[layer : layer + 1], (own_rows, 128))
+
+        def update(i):
+            for n in range(8):
+                cols = pl.ds(pl.multiple_of(i * 1024 + n * 128, 128), 128)
+                updated = w_in[layer, 0, :, cols] - this_factor * gbuf[layer, :, cols]
+                new_weights[layer, 0, :, cols] = updated
+                previous = s_in[layer, 0, :, cols]
+                new_shadow[layer, 0, :, cols] = previous + this_beta * (updated - previous)
+        loop(0, 2 * half_cols // 1024, update)
 
 
 def on_device(activations, out_grads, weights, shadow, counts):
@@ -452,17 +467,12 @@
     f32, bf16 = jnp.float32, jnp.bfloat16
     dma = pltpu.SemaphoreType.DMA
     vmem = pl.BlockSpec(memory_space=pltpu.VMEM)
-    smem = pl.BlockSpec(memory_space=pltpu.SMEM)
     hbm = pl.BlockSpec(memory_space=pl.ANY)
-    grad, factor, beta = pl.pallas_call(
+    return pl.pallas_call(
         kernel,
-        out_shape=(
-            jax.ShapeDtypeStruct((LAYERS, unit // 2, ff), f32),
-            jax.ShapeDtypeStruct((LAYERS,), f32),
-            jax.ShapeDtypeStruct((LAYERS,), f32),
-        ),
-        in_specs=[vmem, hbm, vmem],
-        out_specs=(hbm, smem, smem),
+        out_shape=(pltpu.VMEM(weights.shape, f32), pltpu.VMEM(shadow.shape, f32)),
+        in_specs=[hbm] * 5,
+        out_specs=(vmem, vmem),
         scratch_shapes=[
             pltpu.VMEM((LAYERS, BLOCKS, rows, wide_z), f32),
             pltpu.VMEM((LAYERS, BLOCKS, rows, wide_y), f32),
@@ -478,19 +488,22 @@
             pltpu.VMEM((BLOCKS, tokens, wide_y), f32),
             pltpu.VMEM((LAYERS, tokens, ff // 2), bf16),
             pltpu.VMEM((LAYERS, tokens, ff // 2), bf16),
+            pltpu.VMEM(acts.shape, bf16),
+            pltpu.VMEM(counts.shape, counts.dtype),
+            pltpu.VMEM(weights.shape, f32),
+            pltpu.VMEM(shadow.shape, f32),
             pltpu.VMEM((LAYERS, tokens, rows), f32),
             pltpu.VMEM((LAYERS, tokens, rows), f32),
             pltpu.VMEM((rows, 2 * tokens), f32),
             pltpu.VMEM((LAYERS, rows, 2 * tokens), bf16),
             pltpu.VMEM((LAYERS, unit // 2, ff), f32),
-            pltpu.VMEM((LAYERS, 128), f32),
-            pltpu.VMEM((7, LAYERS, 128), f32),
-            pltpu.VMEM((LAYERS, 128), f32),
-            pltpu.VMEM((31, LAYERS, 128), f32),
-            pltpu.VMEM((LAYERS, 128), f32),
-            pltpu.VMEM((31, LAYERS, 128), f32),
+            pltpu.VMEM((4, LAYERS, 128), f32),
+            pltpu.VMEM((3, LAYERS, 128), f32),
+            pltpu.VMEM((2 * LAYERS, 128), f32),
+            pltpu.VMEM((31, 2 * LAYERS, 128), f32),
             pltpu.VMEM((LAYERS, unit // 2, 128), f32),
             dma((LAYERS, 2, 2)),
+            dma((4,)),
             dma((2,)),
             dma((2, BLOCKS)),
             dma((2,)),
@@ -505,20 +518,13 @@
             dma((LAYERS,)),
             dma((LAYERS,)),
             dma((2,)),
-            dma((2,)),
-            dma((2,)),
-            dma((2,)),
-            dma,
+            dma((2, 3)),
+            dma((2,)),
         ],
         compiler_params=pltpu.CompilerParams(
-            collective_id=0, has_side_effects=True, vmem_limit_bytes=62 * 1024 * 1024
+            collective_id=0, has_side_effects=True, vmem_limit_bytes=58 * 1024 * 1024
         ),
-    )(acts, og, counts)
-    summed = grad[:, None]
-    factor = factor[:, None, None, None]
-    beta = beta[:, None, None, None]
-    updated = weights - factor * summed
-    return updated, shadow + beta * (updated - shadow)
+    )(acts, og, counts, weights, shadow)
 
 
 def solution(mesh):

time: 134 us -> 127 us (0.948)
  Pallas kernels: 130 us -> 124 us
  other arithmetic: 2.65 us -> 0 us
  local copies, waits for them, and re-layouts: 0.01 us -> 1.85 us
    pallas_call x1, Pallas kernels: 130 us -> 124 us  [on_device(): pl.pallas_call(kernel, out_shape=(pltpu.VMEM(weights.shape, f32), pltpu.V...]
    unnamed x1 -> x0, other arithmetic: 2.65 us -> none
    unnamed x4 -> x2, local copies, waits for them, and re-layouts: 0.01 us -> 1.85 us
where the time goes in v4:
time: 127 us
  Pallas kernels  124 us (98%)
  local copies, waits for them, and re-layouts  1.85 us (1%)
    pallas_call x1, Pallas kernels, on_device(): pl.pallas_call(kernel, out_shape=(pltpu.VMEM(weights.shape, f32), pltpu.V...  124 us

profile of v4, /device:TPU:1, one launch (start us, length us, event | category | flops | bytes accessed | tf_op | source)
XLA Modules:
  0.0 126.9 jit_solution(18397262129617810065)
XLA Ops:
  0.6 124.4 %shard_map.68 = (f32[2,1,8,14336]{3,2,1,0:T(8,128)S(1)}, f32[2,1,8,14336]{3,2,1,0:T(8,128)S(1)}) custom-call(bf16[2,128,256]{2,1,0:T(8,128)(2,1)} %bitcast.3, bf16[2,128,14336]{2,1,0:T(8,128)(2,1)} %bitcast.2, s32[2,1,8]{2,1,0:T(1,128)} %counts_in.1, f32[2,1,8,14336]{3,2,1,0:T(8,128)} %weights.1, f32[2,1,8,14336]{3,2,1,0:T(8,128)} %shadow.1), custom_call_target="tpu_custom_call" | custom-call | tf_op jit(solution)/shard_map/pallas_call | solution.py:471
  125.1 0.9 copy.9
  126.0 0.9 copy.10

commit v5 on v4

--- a/solution.py
+++ b/solution.py
@@ -25,7 +25,7 @@
     part_z, part_y, ring_z, ring_y, y_got, y_relay, z_got, z_relay, x_got_z, x_got_y, x_out_z, x_out_y,
     own_half, other_half, acts, counts, w_in, s_in, a_out, a_got, a_rows, a_t, gbuf, c_own, c_got, q_own, q_got, q_acc,
     og_sem, in_sem, x_send, x_recv, x_recv_late, a_sem, ring_send, ring_recv,
-    y_send, y_mid, y_end, y_units, z_send, z_mid, z_end_sem, g_sem, c_sem, q_sem,
+    y_send, y_mid, y_end, y_parts, y_unit, z_send, z_mid, z_end_sem, g_sem, c_sem, q_sem,
 ):
     z = lax.axis_index("dp")
     x = lax.axis_index("expert_0")
@@ -96,13 +96,11 @@
     for device in near:
         pl.semaphore_signal(barrier, inc=1, device_id=device, device_id_type=MESH)
 
+    og_copy(0, 1, Y).start()
     in_copies[0].start()
+    for which, kind in ((0, Y), (1, Z), (0, Z)):
+        og_copy(0, which, kind).start()
     in_copies[1].start()
-    for layer in range(LAYERS):
-        for which, kind in ((1, Y), (0, Y), (1, Z), (0, Z)):
-            og_copy(layer, which, kind).start()
-    in_copies[2].start()
-    in_copies[3].start()
 
     def cols_of(kind, j):
         return pl.ds(pl.multiple_of(first_col[kind] + j * width[kind], 128), width[kind])
@@ -117,51 +115,49 @@
     def x_all(layer, kind):
         return remote(x_out[kind], x_got[kind].at[layer], x_send.at[kind], x_recv_late.at[kind], mate)
 
-    in_copies[0].wait()
-    a_out[...] = acts[...].astype(jnp.float32)
-    in_copies[1].wait()
-    c_own[0] = jnp.zeros_like(c_own[0])
-    c_own[0, :, 0:8] = counts[:, 0, :].astype(jnp.float32)
-    q_acc[...] = jnp.zeros_like(q_acc)
-    og_copy(0, 1, Y).wait()
-    loop(0, 2, lambda j: convert(0, Y, j))
-    pl.semaphore_wait(barrier, len(near))
-
-    a_copy = remote(a_out, a_got, a_sem.at[0], a_sem.at[1], mate)
-    a_copy.start()
-
-    def swap(layer, kind, low, high):
-        def act(j):
-            convert(layer, kind, j)
-            x_copy(layer, kind, j).start()
-        loop(low, high, act)
-
-    loop(0, 2, lambda j: x_copy(0, Y, j).start())
-    og_copy(0, 1, Z).wait()
-    swap(0, Z, 0, 4)
-    swap(0, Y, 2, 4)
-
-    c_copies = [
-        remote(c_own.at[i], c_got.at[i], c_sem.at[0, i], c_sem.at[1, i], device)
-        for i, device in enumerate((near[5], near[6], at(y_lo=1 - y_lo)))
-    ]
-    c_copies[0].start()
-
-    def c_next(i):
-        c_copies[i].wait_recv()
-        c_own[i + 1] = c_own[i] + c_got[i]
-        if i < 2:
-            c_copies[i + 1].start()
-
-    a_copy.wait_recv()
-    for layer in range(LAYERS):
+    def a_copy(layer):
+        return remote(a_out.at[layer], a_got.at[layer], a_sem.at[0, layer], a_sem.at[1, layer], mate)
+
+    def a_join(layer):
         a_rows[:, 0:tokens] = a_out[layer].T
+        a_copy(layer).wait_recv()
         a_rows[:, tokens : 2 * tokens] = a_got[layer].T
         for half in range(2):
             side = y_hi if half == 0 else 1 - y_hi
             for zz in range(NZ):
                 piece = a_rows[pl.ds(pl.multiple_of(zz * 2 * unit + side * unit, unit), unit), :]
                 a_t[layer, half * half_rows + zz * unit : half * half_rows + (zz + 1) * unit, :] = piece.astype(jnp.bfloat16)
+
+    def swap(layer, kind, low, high):
+        def act(j):
+            convert(layer, kind, j)
+            x_copy(layer, kind, j).start()
+        loop(low, high, act)
+
+    c_copies = [
+        remote(c_own.at[i], c_got.at[i], c_sem.at[0, i], c_sem.at[1, i], device)
+        for i, device in enumerate((near[5], near[6], at(y_lo=1 - y_lo)))
+    ]
+
+    def c_next(i):
+        c_copies[i].wait_recv()
+        c_own[i + 1] = c_own[i] + c_got[i]
+        if i < 2:
+            c_copies[i + 1].start()
+
+    og_copy(0, 1, Y).wait()
+    loop(0, 2, lambda j: convert(0, Y, j))
+    in_copies[0].wait()
+    a_out[...] = acts[...].astype(jnp.float32)
+    pl.semaphore_wait(barrier, len(near))
+
+    a_copy(0).start()
+    loop(0, 2, lambda j: x_copy(0, Y, j).start())
+    og_copy(0, 1, Z).wait()
+    swap(0, Z, 0, 4)
+    swap(0, Y, 2, 4)
+    a_copy(1).start()
+    a_join(0)
 
     def multiply(layer, kind, j):
         if layer == 0:
@@ -257,22 +253,32 @@
     def unit_rows(away):
         return pl.ds(pl.multiple_of(lax.rem(z + away + NZ, NZ) * unit, unit), unit)
 
-    def y_forward_units(layer, p):
-        pair(layer, p, y_mid).wait_recv()
-        for g, aways in enumerate(groups):
-            for away in aways:
+    def y_first(layer, j, at_rows, sign, part_of, g):
+        others = pl.ds(pl.multiple_of(half_rows + at_rows.start, unit), unit)
+        return remote(
+            part_y.at[layer, j, others, :], y_relay.at[layer, j, at_rows, :], y_send.at[0], y_parts.at[part_of], y_next(sign)
+        )
+
+    def y_second(layer, j, at_rows, sign, part_of, g):
+        return remote(
+            y_relay.at[layer, j, at_rows, :], y_got.at[layer, j, at_rows, :], y_send.at[1], y_unit.at[g], y_next(sign)
+        )
+
+    def y_units(layer, p, hop, part_of, which):
+        for g in which:
+            for away in groups[g]:
                 def act(j):
                     sign = sign_of(j)
-                    at_rows = unit_rows(sign * away)
-                    remote(
-                        y_relay.at[layer, j, at_rows, :], y_got.at[layer, j, at_rows, :],
-                        y_send.at[1], y_units.at[g], y_next(sign),
-                    ).start()
+                    hop(layer, j, unit_rows(sign * away), sign, part_of, g).start()
                 loop(2 * p, 2 * p + 2, act)
+
+    def y_units_wait(layer, p, part_of, units):
+        these = y_relay.at[layer, 2 * p : 2 * p + 2, 0 : unit * units, :]
+        remote(these, these, y_send.at[0], y_parts.at[part_of], mate).wait_recv()
 
     def y_units_add(layer, p, g):
         four = y_got.at[layer, 2 * p : 2 * p + 2, 0 : unit * len(groups[g]), :]
-        remote(four, four, y_send.at[1], y_units.at[g], mate).wait_recv()
+        remote(four, four, y_send.at[1], y_unit.at[g], mate).wait_recv()
         for away in groups[g]:
             def act(j):
                 at_rows = unit_rows(sign_of(j) * away)
@@ -338,9 +344,9 @@
     def all_of(got, sems):
         return remote(got, got, sems.at[0], sems.at[1], mate)
 
-    def to_y(j):
-        multiply(0, Y, j)
-        y_copy(0, j).start()
+    def to_y(layer, j):
+        multiply(layer, Y, j)
+        y_copy(layer, j).start()
 
     def to_z(j):
         multiply(0, Z, j)
@@ -348,64 +354,82 @@
         chain_start(Z, 0, 2 * j + 1)
 
     og_copy(0, 0, Y).wait()
-    loop(0, 2, to_y)
+    loop(0, 2, lambda j: to_y(0, j))
     og_copy(0, 0, Z).wait()
     loop(0, 4, to_z)
-    loop(2, 4, to_y)
-
-    for kind in (Z, Y):
+    loop(2, 4, lambda j: to_y(0, j))
+
+    for which, kind in ((1, Y), (1, Z), (0, Y), (0, Z)):
+        og_copy(1, which, kind).start()
+    in_copies[1].wait()
+    c_own[0] = jnp.zeros_like(c_own[0])
+    c_own[0, :, 0:8] = counts[:, 0, :].astype(jnp.float32)
+    c_copies[0].start()
+    q_acc[...] = jnp.zeros_like(q_acc)
+    for kind in (Y, Z):
         x_all(0, kind).wait_send()
         og_copy(1, 1, kind).wait()
         swap(1, kind, 0, 4)
+    in_copies[2].start()
+    in_copies[3].start()
+    og_copy(1, 0, Y).wait()
     og_copy(1, 0, Z).wait()
-    og_copy(1, 0, Y).wait()
 
     steps(Z, 0, 0, 8, 1)
+    a_join(1)
+    x_all(1, Y).wait_recv()
+    loop(0, 2, lambda j: to_y(1, j))
     x_all(1, Z).wait_recv()
     loop(0, 4, lambda j: multiply(1, Z, j))
     steps(Z, 0, 0, 8, 2)
     y_forward(0, 0)
-    x_all(1, Y).wait_recv()
-    loop(0, 4, lambda j: multiply(1, Y, j))
+    loop(2, 4, lambda j: multiply(1, Y, j))
     steps(Z, 0, 0, 8, 3)
     starts(Z, 1, 0, 8)
     y_forward(0, 1)
-    loop(0, 4, lambda j: y_copy(1, j).start())
     z_last(0)
     c_next(0)
     steps(Z, 1, 0, 8, 1)
+    y_forward(1, 0)
+    y_units(1, 1, y_first, 0, (0, 1))
+    y_units(1, 1, y_first, 1, (2, 3, 4))
     steps(Z, 1, 0, 8, 2)
     c_next(1)
     steps(Z, 1, 0, 8, 3)
+
     y_begin(0, 0)
     y_begin(0, 1)
     z_last(1)
-    y_forward(1, 0)
     steps(Y, 0, 0, 4, 1)
-    steps(Y, 0, 0, 4, 2)
-    y_forward_units(1, 1)
+    steps(Y, 0, 0, 2, 2)
+    y_begin(1, 0)
+    steps(Y, 0, 2, 4, 2)
+    y_units_wait(1, 1, 0, 4)
+    y_units(1, 1, y_second, 0, (0, 1))
+    steps(Y, 1, 0, 2, 1)
+    steps(Y, 0, 0, 4, 3)
+    y_units_wait(1, 1, 1, 4)
+    y_units(1, 1, y_second, 0, (2,))
     for layer in range(LAYERS):
         loop(0, BLOCKS, lambda j: z_copy(layer, j).start())
-    steps(Y, 0, 0, 4, 3)
-    y_begin(1, 0)
-    y_finish(0, 0, 4)
+    y_units(1, 1, y_second, 0, (3, 4))
 
     y_units_add(1, 1, 0)
     starts(Y, 1, 2, 4)
-    steps(Y, 1, 0, 2, 1)
+    y_finish(0, 0, 4)
+    steps(Y, 1, 0, 2, 2)
     y_units_add(1, 1, 1)
     steps(Y, 1, 2, 4, 1)
-    steps(Y, 1, 0, 2, 2)
+    steps(Y, 1, 0, 2, 3)
     y_units_add(1, 1, 2)
     steps(Y, 1, 2, 4, 2)
+    c_next(2)
     z_forward(0)
     z_forward(1)
-    c_next(2)
-    steps(Y, 1, 0, 2, 3)
+    y_finish(1, 0, 2)
     y_units_add(1, 1, 3)
     steps(Y, 1, 2, 4, 3)
     y_units_add(1, 1, 4)
-    y_finish(1, 0, 2)
     z_finish(0)
     z_finish(1)
     y_finish(1, 2, 4)
@@ -424,11 +448,12 @@
 
     all_g.wait_send()
     for i in range(2):
-        remote(y_relay, y_got, y_send.at[i], y_units.at[0], mate).wait_send()
+        remote(y_relay, y_got, y_send.at[i], y_unit.at[0], mate).wait_send()
         remote(z_relay, z_got, z_send.at[i], z_mid.at[0], mate).wait_send()
     for kind in (Z, Y):
         x_all(1, kind).wait_send()
-    a_copy.wait_send()
+    for layer in range(LAYERS):
+        a_copy(layer).wait_send()
     for copy in c_copies:
         copy.wait_send()
     all_of(q_got, q_sem).wait_send()
@@ -456,6 +481,18 @@
         loop(0, 2 * half_cols // 1024, update)
 
 
+def writer(updated, smoothed, new_weights, new_shadow, sems):
+    copies = [
+        pltpu.make_async_copy(src.at[layer], dst.at[layer], sems.at[i, layer])
+        for i, (src, dst) in enumerate(((updated, new_weights), (smoothed, new_shadow)))
+        for layer in range(LAYERS)
+    ]
+    for copy in copies:
+        copy.start()
+    for copy in copies:
+        copy.wait()
+
+
 def on_device(activations, out_grads, weights, shadow, counts):
     acts, og = activations[:, 0], out_grads[:, 0]
     tokens, rows = acts.shape[1:]
@@ -468,7 +505,7 @@
     dma = pltpu.SemaphoreType.DMA
     vmem = pl.BlockSpec(memory_space=pltpu.VMEM)
     hbm = pl.BlockSpec(memory_space=pl.ANY)
-    return pl.pallas_call(
+    updated, smoothed = pl.pallas_call(
         kernel,
         out_shape=(pltpu.VMEM(weights.shape, f32), pltpu.VMEM(shadow.shape, f32)),
         in_specs=[hbm] * 5,
@@ -507,12 +544,13 @@
             dma((2,)),
             dma((2, BLOCKS)),
             dma((2,)),
-            dma((2,)),
+            dma((2, LAYERS)),
             dma((16,)),
             dma((16, 2)),
             dma((2,)),
             dma((LAYERS, 2)),
             dma((LAYERS, 2)),
+            dma((2,)),
             dma((5,)),
             dma((2,)),
             dma((LAYERS,)),
@@ -525,6 +563,13 @@
             collective_id=0, has_side_effects=True, vmem_limit_bytes=58 * 1024 * 1024
         ),
     )(acts, og, counts, weights, shadow)
+    return pl.pallas_call(
+        writer,
+        out_shape=(jax.ShapeDtypeStruct(weights.shape, f32), jax.ShapeDtypeStruct(shadow.shape, f32)),
+        in_specs=[vmem, vmem],
+        out_specs=(hbm, hbm),
+        scratch_shapes=[dma((2, LAYERS))],
+    )(*(pltpu.with_memory_space_constraint(a, pltpu.VMEM) for a in (updated, smoothed)))
 
 
 def solution(mesh):

time: 127 us -> 125 us (0.984)
  local copies, waits for them, and re-layouts: 1.85 us -> 0 us
    unnamed x2 -> x0, local copies, waits for them, and re-layouts: 1.85 us -> none
where the time goes in v5:
time: 125 us
  Pallas kernels  125 us (100%)
    pallas_call x1, Pallas kernels, on_device(): pl.pallas_call(kernel, out_shape=(pltpu.VMEM(weights.shape, f32), pltpu.V...  123 us

profile of v5, /device:TPU:1, one launch (start us, length us, event | category | flops | bytes accessed | tf_op | source)
XLA Modules:
  0.0 125.4 jit_solution(2152475494525920682)
XLA Ops:
  0.6 123.5 %shard_map.68 = (f32[2,1,8,14336]{3,2,1,0:T(8,128)S(1)}, f32[2,1,8,14336]{3,2,1,0:T(8,128)S(1)}) custom-call(bf16[2,128,256]{2,1,0:T(8,128)(2,1)} %bitcast.3, bf16[2,128,14336]{2,1,0:T(8,128)(2,1)} %bitcast.2, s32[2,1,8]{2,1,0:T(1,128)} %counts_in.1, f32[2,1,8,14336]{3,2,1,0:T(8,128)} %weights.1, f32[2,1,8,14336]{3,2,1,0:T(8,128)} %shadow.1), custom_call_target="tpu_custom_call" | custom-call | tf_op jit(solution)/shard_map/pallas_call | solution.py:508
  124.1 1.3 %shard_map.69 = (f32[2,1,8,14336]{3,2,1,0:T(8,128)}, f32[2,1,8,14336]{3,2,1,0:T(8,128)}) custom-call(f32[2,1,8,14336]{3,2,1,0:T(8,128)S(1)} %get-tuple-element.4.updated, f32[2,1,8,14336]{3,2,1,0:T(8,128)S(1)} %get-tuple-element.5.smoothed), custom_call_target="tpu_custom_call" | custom-call | tf_op jit(solution)/shard_map/pallas_call | solution.py:566

commit v6 on v5

--- a/solution.py
+++ b/solution.py
@@ -17,7 +17,7 @@
 
 NZ = 8
 BLOCKS = 4
-Z, Y = 0, 1
+Z, Y, YH = 0, 1, 2
 
 
 def kernel(
@@ -38,11 +38,11 @@
     half_rows = rows // 2
     unit = half_rows // NZ
     own_rows = unit // 2
-    part = (part_z, part_y)
-    ring = (ring_z, ring_y)
+    part = (part_z, part_y, part_y)
+    ring = (ring_z, ring_y, ring_y)
     x_got = (x_got_z, x_got_y)
     x_out = (x_out_z, x_out_y)
-    width = (part_z.shape[-1], part_y.shape[-1])
+    width = (part_z.shape[-1], part_y.shape[-1], part_y.shape[-1] // 2)
     first_col = (0, BLOCKS * width[Z])
     half_cols = BLOCKS * (width[Z] + width[Y])
 
@@ -75,13 +75,15 @@
             return 0
         lax.fori_loop(low, high, body, 0)
 
-    def og_copy(layer, which, kind):
+    pieces = ((0, 4 * width[Z]), (first_col[Y], 2 * width[Y]), (first_col[Y] + 2 * width[Y], 2 * width[Y]))
+
+    def og_copy(layer, which, piece):
         first = core if which == 0 else 1 - core
         to = own_half if which == 0 else other_half
-        size = BLOCKS * width[kind]
-        cols = pl.ds(pl.multiple_of(first * half_cols + first_col[kind], 128), size)
+        begin, size = pieces[piece]
+        cols = pl.ds(pl.multiple_of(first * half_cols + begin, 128), size)
         return pltpu.make_async_copy(
-            og.at[layer, :, cols], to.at[layer, :, first_col[kind] : first_col[kind] + size], og_sem.at[layer, which, kind]
+            og.at[layer, :, cols], to.at[layer, :, begin : begin + size], og_sem.at[layer, which, piece]
         )
 
     in_copies = [
@@ -96,10 +98,10 @@
     for device in near:
         pl.semaphore_signal(barrier, inc=1, device_id=device, device_id_type=MESH)
 
-    og_copy(0, 1, Y).start()
+    og_copy(0, 1, 1).start()
     in_copies[0].start()
-    for which, kind in ((0, Y), (1, Z), (0, Z)):
-        og_copy(0, which, kind).start()
+    for which, piece in ((0, 1), (1, 0), (0, 0), (1, 2), (0, 2)):
+        og_copy(0, which, piece).start()
     in_copies[1].start()
 
     def cols_of(kind, j):
@@ -109,8 +111,15 @@
         x_out[kind][j] = other_half[layer, :, cols_of(kind, j)].astype(jnp.float32)
 
     def x_copy(layer, kind, j):
-        sem = x_recv.at[kind, j] if layer == 0 else x_recv_late.at[kind]
+        sem = x_recv.at[4 * kind + j] if layer == 0 else x_recv_late.at[kind]
         return remote(x_out[kind].at[j], x_got[kind].at[layer, j], x_send.at[kind], sem, mate)
+
+    def half_cols_of(h):
+        return pl.ds(h * width[YH], width[YH])
+
+    def x_half(j, h):
+        cols = half_cols_of(h)
+        return remote(x_out_y.at[j, :, cols], x_got_y.at[0, j, :, cols], x_send.at[Y], x_recv.at[4 + j + 4 * h], mate)
 
     def x_all(layer, kind):
         return remote(x_out[kind], x_got[kind].at[layer], x_send.at[kind], x_recv_late.at[kind], mate)
@@ -145,16 +154,19 @@
         if i < 2:
             c_copies[i + 1].start()
 
-    og_copy(0, 1, Y).wait()
+    og_copy(0, 1, 1).wait()
     loop(0, 2, lambda j: convert(0, Y, j))
     in_copies[0].wait()
     a_out[...] = acts[...].astype(jnp.float32)
     pl.semaphore_wait(barrier, len(near))
 
     a_copy(0).start()
-    loop(0, 2, lambda j: x_copy(0, Y, j).start())
-    og_copy(0, 1, Z).wait()
-    swap(0, Z, 0, 4)
+    loop(0, 2, lambda j: x_half(j, 0).start())
+    og_copy(0, 1, 0).wait()
+    swap(0, Z, 0, 2)
+    loop(0, 2, lambda j: x_half(j, 1).start())
+    swap(0, Z, 2, 4)
+    og_copy(0, 1, 2).wait()
     swap(0, Y, 2, 4)
     a_copy(1).start()
     a_join(0)
@@ -167,57 +179,62 @@
         part[kind][layer, j] = jnp.dot(a_t[layer], both, preferred_element_type=jnp.float32)
 
     def stream(kind, layer, slot):
+        full = pl.ds(0, width[kind])
         if kind == Z:
-            return slot // 2, lax.rem(slot, 2), layer * 8 + slot, layer * 8 + slot
-        return slot, 0, layer * 4 + slot, layer * 4 + slot
+            return slot // 2, lax.rem(slot, 2), layer * 8 + slot, layer * 8 + slot, full
+        if kind == Y:
+            return slot, 0, layer * 4 + slot, layer * 4 + slot, full
+        j = 2 + lax.rem(slot, 2)
+        cols = pl.ds(pl.multiple_of(slot // 2 * width[YH], 128), width[YH])
+        return j, 0, layer * 4 + j, layer * 4 + 2 + slot, cols
 
     def sign_of(slot):
         return 1 - 2 * lax.rem(slot, 2)
 
-    def chunk(kind, layer, j, half, away):
+    def chunk(kind, layer, slot, away):
+        j, half, _, _, cols = stream(kind, layer, slot)
         index = lax.rem(z + away + NZ, NZ)
-        return part[kind].at[layer, j, pl.ds(pl.multiple_of(half * half_rows + index * unit, unit), unit), :]
+        return part[kind].at[layer, j, pl.ds(pl.multiple_of(half * half_rows + index * unit, unit), unit), cols]
 
     def long_copy(kind, layer, slot, step):
-        j, half, k, sem = stream(kind, layer, slot)
+        _, _, k, sem, cols = stream(kind, layer, slot)
         sign = sign_of(slot)
-        src = chunk(kind, layer, j, half, sign * 4) if step == 0 else ring[kind].at[k, step - 1]
-        return remote(src, ring[kind].at[k, step], ring_send.at[sem], ring_recv.at[sem, step % 2], z_next(sign))
+        src = chunk(kind, layer, slot, sign * 4) if step == 0 else ring[kind].at[k, step - 1, :, cols]
+        dst = ring[kind].at[k, step, :, cols]
+        return remote(src, dst, ring_send.at[min(kind, Y)], ring_recv.at[sem, step % 2], z_next(sign))
 
     def short_copy(kind, layer, slot, step):
-        j, half, k, sem = stream(kind, layer, slot)
+        _, _, k, sem, cols = stream(kind, layer, slot)
         sign = sign_of(slot)
-        src = chunk(kind, layer, j, half, sign * -3) if step == 0 else ring[kind].at[k, 4 + step - 1]
-        return remote(src, ring[kind].at[k, 4 + step], ring_send.at[sem], ring_recv.at[sem, step % 2], z_next(-sign))
+        src = chunk(kind, layer, slot, sign * -3) if step == 0 else ring[kind].at[k, 3 + step, :, cols]
+        dst = ring[kind].at[k, 4 + step, :, cols]
+        return remote(src, dst, ring_send.at[min(kind, Y)], ring_recv.at[sem, step % 2], z_next(-sign))
 
     def both_of(kind, layer, slot, step):
-        _, _, k, sem = stream(kind, layer, slot)
-        two = ring[kind].at[k, 0:2]
-        return remote(two, two, ring_send.at[sem], ring_recv.at[sem, step % 2], z_next(1))
+        _, _, k, sem, cols = stream(kind, layer, slot)
+        two = ring[kind].at[k, 0:2, :, cols]
+        return remote(two, two, ring_send.at[min(kind, Y)], ring_recv.at[sem, step % 2], z_next(1))
 
     def chain_start(kind, layer, slot):
         long_copy(kind, layer, slot, 0).start()
         short_copy(kind, layer, slot, 0).start()
 
     def chain_step(kind, layer, slot, step):
-        j, half, k, _ = stream(kind, layer, slot)
+        _, _, k, _, cols = stream(kind, layer, slot)
+        held = ring[kind]
         sign = sign_of(slot)
-        before = both_of(kind, layer, slot, step - 1)
-        before.wait_recv()
-        ring[kind][k, step - 1] = ring[kind][k, step - 1] + chunk(kind, layer, j, half, sign * (4 - step))[...]
+        both_of(kind, layer, slot, step - 1).wait_recv()
+        held[k, step - 1, :, cols] = held[k, step - 1, :, cols] + chunk(kind, layer, slot, sign * (4 - step))[...]
         if step < 3:
-            ring[kind][k, 3 + step] = ring[kind][k, 3 + step] + chunk(kind, layer, j, half, sign * (step - 3))[...]
-        before.wait_send()
+            held[k, 3 + step, :, cols] = held[k, 3 + step, :, cols] + chunk(kind, layer, slot, sign * (step - 3))[...]
         long_copy(kind, layer, slot, step).start()
         if step < 3:
             short_copy(kind, layer, slot, step).start()
 
     def chain_last(kind, layer, slot):
-        j, half, k, _ = stream(kind, layer, slot)
-        before = long_copy(kind, layer, slot, 3)
-        before.wait_recv()
-        before.wait_send()
-        return k, ring[kind][k, 3] + chunk(kind, layer, j, half, 0)[...]
+        _, _, k, _, cols = stream(kind, layer, slot)
+        long_copy(kind, layer, slot, 3).wait_recv()
+        return ring[kind][k, 3, :, cols] + chunk(kind, layer, slot, 0)[...] + ring[kind][k, 6, :, cols]
 
     def steps(kind, layer, low, high, step):
         loop(low, high, lambda slot: chain_step(kind, layer, slot, step))
@@ -227,8 +244,7 @@
 
     def z_last(layer):
         def act(slot):
-            k, value = chain_last(Z, layer, slot)
-            ring_z[k, 3] = value + ring_z[k, 6]
+            ring_z[layer * 8 + slot, 3] = chain_last(Z, layer, slot)
         loop(0, 8, act)
 
     def y_copy(layer, j):
@@ -308,15 +324,20 @@
         z_all(layer, z_mid).wait_recv()
         loop(0, BLOCKS, lambda j: z_pass(layer, j).start())
 
-    def gcols(side, kind, j):
-        return pl.ds(pl.multiple_of(side * half_cols + first_col[kind] + j * width[kind], 128), width[kind])
-
-    def finish(kind, layer, j, k, value):
-        ring[kind][k, 3] = value
-        src = ring[kind].at[k, 3, pl.ds(pl.multiple_of((1 - core) * own_rows, own_rows), own_rows), :]
-        remote(src, gbuf.at[layer, :, gcols(core, kind, j)], g_sem.at[0], g_sem.at[1], mate).start()
-        mine = ring[kind][k, 3, pl.ds(pl.multiple_of(core * own_rows, own_rows), own_rows), :]
-        gbuf[layer, :, gcols(core, kind, j)] = mine
+    def finish(kind, layer, slot, value):
+        j, _, k, _, cols = stream(kind, layer, slot)
+        held = ring[kind]
+        held[k, 3, :, cols] = value
+        col = core * half_cols + first_col[min(kind, Y)] + j * width[min(kind, Y)] + cols.start
+        where = pl.ds(pl.multiple_of(col, 128), width[kind])
+
+        def of(c):
+            return pl.ds(pl.multiple_of(c * own_rows, own_rows), own_rows)
+
+        remote(
+            held.at[k, 3, of(1 - core), cols], gbuf.at[layer, :, where], g_sem.at[0], g_sem.at[1], mate
+        ).start()
+        gbuf[layer, :, where] = held[k, 3, of(core), cols]
         squares = value * value
         folded = squares[0:own_rows] + squares[own_rows : 2 * own_rows]
         total = folded[:, 0:128]
@@ -326,17 +347,10 @@
 
     def z_finish(layer):
         z_all(layer, z_end_sem).wait_recv()
-
-        def act(j):
-            k = layer * 8 + j * 2
-            finish(Z, layer, j, k, ring_z[k, 3] + z_got[layer, j])
-        loop(0, BLOCKS, act)
-
-    def y_finish(layer, low, high):
-        def act(j):
-            k, value = chain_last(Y, layer, j)
-            finish(Y, layer, j, k, value + ring_y[k, 6])
-        loop(low, high, act)
+        loop(0, BLOCKS, lambda j: finish(Z, layer, 2 * j, ring_z[layer * 8 + 2 * j, 3] + z_got[layer, j]))
+
+    def y_finish(layer, low, high, kind=Y):
+        loop(low, high, lambda slot: finish(kind, layer, slot, chain_last(kind, layer, slot)))
 
     def q_copy(offset):
         return remote(q_own, q_got.at[offset - 1], q_sem.at[0], q_sem.at[1], group_device(offset))
@@ -353,14 +367,29 @@
         chain_start(Z, 0, 2 * j)
         chain_start(Z, 0, 2 * j + 1)
 
-    og_copy(0, 0, Y).wait()
-    loop(0, 2, lambda j: to_y(0, j))
-    og_copy(0, 0, Z).wait()
-    loop(0, 4, to_z)
+    def to_y_half(j, h):
+        cols = half_cols_of(h)
+        x_half(j, h).wait_recv()
+        mine = own_half[0, :, pl.ds(pl.multiple_of(first_col[Y] + j * width[Y] + h * width[YH], 128), width[YH])]
+        both = jnp.concatenate([mine, x_got_y[0, j, :, cols].astype(jnp.bfloat16)], axis=0)
+        part_y[0, j, :, cols] = jnp.dot(a_t[0], both, preferred_element_type=jnp.float32)
+        remote(
+            part_y.at[0, j, pl.ds(half_rows, half_rows), cols], y_relay.at[0, j, :, cols],
+            y_send.at[0], y_mid.at[0, 0], y_next(sign_of(j)),
+        ).start()
+
+    og_copy(0, 0, 1).wait()
+    loop(0, 2, lambda j: to_y_half(j, 0))
+    og_copy(0, 0, 0).wait()
+    loop(0, 2, to_z)
+    loop(0, 2, lambda j: to_y_half(j, 1))
+    loop(2, 4, to_z)
+    og_copy(0, 0, 2).wait()
     loop(2, 4, lambda j: to_y(0, j))
 
-    for which, kind in ((1, Y), (1, Z), (0, Y), (0, Z)):
-        og_copy(1, which, kind).start()
+    for which in (1, 0):
+        for piece in (1, 2, 0):
+            og_copy(1, which, piece).start()
     in_copies[1].wait()
     c_own[0] = jnp.zeros_like(c_own[0])
     c_own[0, :, 0:8] = counts[:, 0, :].astype(jnp.float32)
@@ -368,12 +397,13 @@
     q_acc[...] = jnp.zeros_like(q_acc)
     for kind in (Y, Z):
         x_all(0, kind).wait_send()
-        og_copy(1, 1, kind).wait()
+        for piece in ((0,), (1, 2))[kind]:
+            og_copy(1, 1, piece).wait()
         swap(1, kind, 0, 4)
     in_copies[2].start()
     in_copies[3].start()
-    og_copy(1, 0, Y).wait()
-    og_copy(1, 0, Z).wait()
+    for piece in range(3):
+        og_copy(1, 0, piece).wait()
 
     steps(Z, 0, 0, 8, 1)
     a_join(1)
@@ -401,38 +431,40 @@
     y_begin(0, 1)
     z_last(1)
     steps(Y, 0, 0, 4, 1)
+    y_begin(1, 0)
     steps(Y, 0, 0, 2, 2)
-    y_begin(1, 0)
-    steps(Y, 0, 2, 4, 2)
     y_units_wait(1, 1, 0, 4)
     y_units(1, 1, y_second, 0, (0, 1))
     steps(Y, 1, 0, 2, 1)
-    steps(Y, 0, 0, 4, 3)
+    steps(Y, 0, 2, 4, 2)
     y_units_wait(1, 1, 1, 4)
     y_units(1, 1, y_second, 0, (2,))
     for layer in range(LAYERS):
         loop(0, BLOCKS, lambda j: z_copy(layer, j).start())
     y_units(1, 1, y_second, 0, (3, 4))
+    steps(Y, 1, 0, 2, 2)
 
     y_units_add(1, 1, 0)
-    starts(Y, 1, 2, 4)
-    y_finish(0, 0, 4)
-    steps(Y, 1, 0, 2, 2)
+    starts(YH, 1, 0, 4)
+    steps(Y, 0, 0, 2, 3)
     y_units_add(1, 1, 1)
-    steps(Y, 1, 2, 4, 1)
+    steps(YH, 1, 0, 4, 1)
+    steps(Y, 0, 2, 4, 3)
     steps(Y, 1, 0, 2, 3)
+    y_finish(0, 0, 2)
     y_units_add(1, 1, 2)
-    steps(Y, 1, 2, 4, 2)
-    c_next(2)
+    steps(YH, 1, 0, 4, 2)
     z_forward(0)
     z_forward(1)
+    c_next(2)
+    y_units_add(1, 1, 3)
+    steps(YH, 1, 0, 4, 3)
+    y_finish(0, 2, 4)
     y_finish(1, 0, 2)
-    y_units_add(1, 1, 3)
-    steps(Y, 1, 2, 4, 3)
+    z_finish(0)
     y_units_add(1, 1, 4)
-    z_finish(0)
+    y_finish(1, 0, 4, YH)
     z_finish(1)
-    y_finish(1, 2, 4)
 
     q_own[0:2] = jnp.sum(q_acc[...], axis=1)
     q_own[2:4] = c_own[3]
@@ -452,6 +484,7 @@
         remote(z_relay, z_got, z_send.at[i], z_mid.at[0], mate).wait_send()
     for kind in (Z, Y):
         x_all(1, kind).wait_send()
+        remote(ring[kind], ring[kind], ring_send.at[kind], ring_recv.at[0, 0], mate).wait_send()
     for layer in range(LAYERS):
         a_copy(layer).wait_send()
     for copy in c_copies:
@@ -539,13 +572,13 @@
             pltpu.VMEM((2 * LAYERS, 128), f32),
             pltpu.VMEM((31, 2 * LAYERS, 128), f32),
             pltpu.VMEM((LAYERS, unit // 2, 128), f32),
-            dma((LAYERS, 2, 2)),
+            dma((LAYERS, 2, 3)),
             dma((4,)),
             dma((2,)),
-            dma((2, BLOCKS)),
+            dma((10,)),
             dma((2,)),
             dma((2, LAYERS)),
-            dma((16,)),
+            dma((2,)),
             dma((16, 2)),
             dma((2,)),
             dma((LAYERS, 2)),

time: 125 us -> 125 us (level)
  no operation moved by 1% of the time
where the time goes in v6:
time: 125 us
  Pallas kernels  124 us (99%)
    pallas_call x1, Pallas kernels, on_device(): pl.pallas_call(kernel, out_shape=(pltpu.VMEM(weights.shape, f32), pltpu.V...  123 us

profile of v6, /device:TPU:1, one launch (start us, length us, event | category | flops | bytes accessed | tf_op | source)
XLA Modules:
  0.0 124.6 jit_solution(4610096763470847083)
XLA Ops:
  0.6 122.7 %shard_map.68 = (f32[2,1,8,14336]{3,2,1,0:T(8,128)S(1)}, f32[2,1,8,14336]{3,2,1,0:T(8,128)S(1)}) custom-call(bf16[2,128,256]{2,1,0:T(8,128)(2,1)} %bitcast.3, bf16[2,128,14336]{2,1,0:T(8,128)(2,1)} %bitcast.2, s32[2,1,8]{2,1,0:T(1,128)} %counts_in.1, f32[2,1,8,14336]{3,2,1,0:T(8,128)} %weights.1, f32[2,1,8,14336]{3,2,1,0:T(8,128)} %shadow.1), custom_call_target="tpu_custom_call" | custom-call | tf_op jit(solution)/shard_map/pallas_call | solution.py:541
  123.3 1.3 %shard_map.69 = (f32[2,1,8,14336]{3,2,1,0:T(8,128)}, f32[2,1,8,14336]{3,2,1,0:T(8,128)}) custom-call(f32[2,1,8,14336]{3,2,1,0:T(8,128)S(1)} %get-tuple-element.4.updated, f32[2,1,8,14336]{3,2,1,0:T(8,128)S(1)} %get-tuple-element.5.smoothed), custom_call_target="tpu_custom_call" | custom-call | tf_op jit(solution)/shard_map/pallas_call | solution.py:599

commit v7 on v6

--- a/solution.py
+++ b/solution.py
@@ -114,8 +114,10 @@
         sem = x_recv.at[4 * kind + j] if layer == 0 else x_recv_late.at[kind]
         return remote(x_out[kind].at[j], x_got[kind].at[layer, j], x_send.at[kind], sem, mate)
 
+    quarter = width[YH] // 2
+
     def half_cols_of(h):
-        return pl.ds(h * width[YH], width[YH])
+        return pl.ds(h * quarter, quarter if h == 0 else width[Y] - quarter)
 
     def x_half(j, h):
         cols = half_cols_of(h)
@@ -370,7 +372,7 @@
     def to_y_half(j, h):
         cols = half_cols_of(h)
         x_half(j, h).wait_recv()
-        mine = own_half[0, :, pl.ds(pl.multiple_of(first_col[Y] + j * width[Y] + h * width[YH], 128), width[YH])]
+        mine = own_half[0, :, pl.ds(pl.multiple_of(first_col[Y] + j * width[Y] + cols.start, 128), cols.size)]
         both = jnp.concatenate([mine, x_got_y[0, j, :, cols].astype(jnp.bfloat16)], axis=0)
         part_y[0, j, :, cols] = jnp.dot(a_t[0], both, preferred_element_type=jnp.float32)
         remote(
@@ -420,9 +422,8 @@
     z_last(0)
     c_next(0)
     steps(Z, 1, 0, 8, 1)
+    y_units(1, 1, y_first, 0, (0, 1, 2))
     y_forward(1, 0)
-    y_units(1, 1, y_first, 0, (0, 1))
-    y_units(1, 1, y_first, 1, (2, 3, 4))
     steps(Z, 1, 0, 8, 2)
     c_next(1)
     steps(Z, 1, 0, 8, 3)
@@ -431,39 +432,37 @@
     y_begin(0, 1)
     z_last(1)
     steps(Y, 0, 0, 4, 1)
-    y_begin(1, 0)
-    steps(Y, 0, 0, 2, 2)
-    y_units_wait(1, 1, 0, 4)
-    y_units(1, 1, y_second, 0, (0, 1))
-    steps(Y, 1, 0, 2, 1)
-    steps(Y, 0, 2, 4, 2)
-    y_units_wait(1, 1, 1, 4)
-    y_units(1, 1, y_second, 0, (2,))
+    y_units_wait(1, 1, 0, 6)
+    y_units(1, 1, y_second, 0, (0, 1, 2))
+    y_units(1, 1, y_first, 1, (3, 4))
     for layer in range(LAYERS):
         loop(0, BLOCKS, lambda j: z_copy(layer, j).start())
+    steps(Y, 0, 0, 4, 2)
+    steps(Y, 0, 0, 2, 3)
+    y_begin(1, 0)
+    y_units_add(1, 1, 0)
+    starts(YH, 1, 0, 4)
+    steps(Y, 1, 0, 2, 1)
+    y_units_add(1, 1, 1)
+    steps(YH, 1, 0, 4, 1)
+    y_units_wait(1, 1, 1, 2)
     y_units(1, 1, y_second, 0, (3, 4))
     steps(Y, 1, 0, 2, 2)
-
-    y_units_add(1, 1, 0)
-    starts(YH, 1, 0, 4)
-    steps(Y, 0, 0, 2, 3)
-    y_units_add(1, 1, 1)
-    steps(YH, 1, 0, 4, 1)
-    steps(Y, 0, 2, 4, 3)
-    steps(Y, 1, 0, 2, 3)
-    y_finish(0, 0, 2)
     y_units_add(1, 1, 2)
     steps(YH, 1, 0, 4, 2)
     z_forward(0)
+    steps(Y, 1, 0, 2, 3)
     z_forward(1)
     c_next(2)
     y_units_add(1, 1, 3)
     steps(YH, 1, 0, 4, 3)
-    y_finish(0, 2, 4)
+    steps(Y, 0, 2, 4, 3)
+    y_finish(0, 0, 2)
     y_finish(1, 0, 2)
     z_finish(0)
     y_units_add(1, 1, 4)
     y_finish(1, 0, 4, YH)
+    y_finish(0, 2, 4)
     z_finish(1)
 
     q_own[0:2] = jnp.sum(q_acc[...], axis=1)

time: 125 us -> 123 us (0.984)
    pallas_call x1, Pallas kernels: 123 us -> 121 us  [on_device(): pl.pallas_call(kernel, out_shape=(pltpu.VMEM(weights.shape, f32), pltpu.V...]
where the time goes in v7:
time: 123 us
  Pallas kernels  123 us (100%)
    pallas_call x1, Pallas kernels, on_device(): pl.pallas_call(kernel, out_shape=(pltpu.VMEM(weights.shape, f32), pltpu.V...  121 us

profile of v7, /device:TPU:1, one launch (start us, length us, event | category | flops | bytes accessed | tf_op | source)
XLA Modules:
  0.0 123.2 jit_solution(17522089773494640150)
XLA Ops:
  0.6 121.3 %shard_map.68 = (f32[2,1,8,14336]{3,2,1,0:T(8,128)S(1)}, f32[2,1,8,14336]{3,2,1,0:T(8,128)S(1)}) custom-call(bf16[2,128,256]{2,1,0:T(8,128)(2,1)} %bitcast.3, bf16[2,128,14336]{2,1,0:T(8,128)(2,1)} %bitcast.2, s32[2,1,8]{2,1,0:T(1,128)} %counts_in.1, f32[2,1,8,14336]{3,2,1,0:T(8,128)} %weights.1, f32[2,1,8,14336]{3,2,1,0:T(8,128)} %shadow.1), custom_call_target="tpu_custom_call" | custom-call | tf_op jit(solution)/shard_map/pallas_call | solution.py:540
  121.9 1.3 %shard_map.69 = (f32[2,1,8,14336]{3,2,1,0:T(8,128)}, f32[2,1,8,14336]{3,2,1,0:T(8,128)}) custom-call(f32[2,1,8,14336]{3,2,1,0:T(8,128)S(1)} %get-tuple-element.4.updated, f32[2,1,8,14336]{3,2,1,0:T(8,128)S(1)} %get-tuple-element.5.smoothed), custom_call_target="tpu_custom_call" | custom-call | tf_op jit(solution)/shard_map/pallas_call | solution.py:598

commit v8 on v7

--- a/solution.py
+++ b/solution.py
@@ -21,9 +21,9 @@
 
 
 def kernel(
-    acts_in, og, counts_in, weights, shadow, new_weights, new_shadow,
+    acts_in, og, counts_in, weights, shadow, gbuf, w_in, s_in, scalars,
     part_z, part_y, ring_z, ring_y, y_got, y_relay, z_got, z_relay, x_got_z, x_got_y, x_out_z, x_out_y,
-    own_half, other_half, acts, counts, w_in, s_in, a_out, a_got, a_rows, a_t, gbuf, c_own, c_got, q_own, q_got, q_acc,
+    own_half, other_half, acts, counts, a_out, a_got, a_rows, a_t, c_own, c_got, q_own, q_got, q_acc,
     og_sem, in_sem, x_send, x_recv, x_recv_late, a_sem, ring_send, ring_recv,
     y_send, y_mid, y_end, y_parts, y_unit, z_send, z_mid, z_end_sem, g_sem, c_sem, q_sem,
 ):
@@ -455,15 +455,17 @@
     z_forward(1)
     c_next(2)
     y_units_add(1, 1, 3)
-    steps(YH, 1, 0, 4, 3)
+    steps(YH, 1, 0, 2, 3)
     steps(Y, 0, 2, 4, 3)
+    steps(YH, 1, 2, 4, 3)
     y_finish(0, 0, 2)
     y_finish(1, 0, 2)
     z_finish(0)
     y_units_add(1, 1, 4)
-    y_finish(1, 0, 4, YH)
+    y_finish(1, 0, 2, YH)
     y_finish(0, 2, 4)
     z_finish(1)
+    y_finish(1, 2, 4, YH)
 
     q_own[0:2] = jnp.sum(q_acc[...], axis=1)
     q_own[2:4] = c_own[3]
@@ -499,28 +501,36 @@
     own_load = jnp.sum(jnp.where(lanes == me_expert, totals, 0.0), axis=1, keepdims=True)
     factor = step_size * (own_load / mean_load) * clip_level / jnp.maximum(root_mean, clip_level)
     beta = own_load / (own_load + mean_load)
+    scalars[0:2] = jnp.broadcast_to(factor, (LAYERS, 128))
+    scalars[2:4] = jnp.broadcast_to(beta, (LAYERS, 128))
+
+
+def update(summed, weights, shadow, scalars, new_weights, new_shadow, w_out, s_out, sems):
+    rows, ff = summed.shape[1:]
+    pieces = 2
+    copies = []
     for layer in range(LAYERS):
-        this_factor = jnp.broadcast_to(factor[layer : layer + 1], (own_rows, 128))
-        this_beta = jnp.broadcast_to(beta[layer : layer + 1], (own_rows, 128))
-
-        def update(i):
-            for n in range(8):
-                cols = pl.ds(pl.multiple_of(i * 1024 + n * 128, 128), 128)
-                updated = w_in[layer, 0, :, cols] - this_factor * gbuf[layer, :, cols]
-                new_weights[layer, 0, :, cols] = updated
-                previous = s_in[layer, 0, :, cols]
-                new_shadow[layer, 0, :, cols] = previous + this_beta * (updated - previous)
-        loop(0, 2 * half_cols // 1024, update)
-
-
-def writer(updated, smoothed, new_weights, new_shadow, sems):
-    copies = [
-        pltpu.make_async_copy(src.at[layer], dst.at[layer], sems.at[i, layer])
-        for i, (src, dst) in enumerate(((updated, new_weights), (smoothed, new_shadow)))
-        for layer in range(LAYERS)
-    ]
-    for copy in copies:
-        copy.start()
+        factor = jnp.broadcast_to(scalars[layer : layer + 1, :], (rows, 128))
+        beta = jnp.broadcast_to(scalars[LAYERS + layer : LAYERS + layer + 1, :], (rows, 128))
+        for piece in range(pieces):
+
+            def some(i, _):
+                for n in range(8):
+                    cols = pl.ds(pl.multiple_of(piece * (ff // pieces) + i * 1024 + n * 128, 128), 128)
+                    updated = weights[layer, 0, :, cols] - factor * summed[layer, :, cols]
+                    w_out[layer, 0, :, cols] = updated
+                    previous = shadow[layer, 0, :, cols]
+                    s_out[layer, 0, :, cols] = previous + beta * (updated - previous)
+                return 0
+
+            lax.fori_loop(0, ff // pieces // 1024, some, 0)
+            cols = pl.ds(piece * (ff // pieces), ff // pieces)
+            for i, (src, dst) in enumerate(((w_out, new_weights), (s_out, new_shadow))):
+                copy = pltpu.make_async_copy(
+                    src.at[layer, 0, :, cols], dst.at[layer, 0, :, cols], sems.at[i, layer, piece]
+                )
+                copy.start()
+                copies.append(copy)
     for copy in copies:
         copy.wait()
 
@@ -537,11 +547,16 @@
     dma = pltpu.SemaphoreType.DMA
     vmem = pl.BlockSpec(memory_space=pltpu.VMEM)
     hbm = pl.BlockSpec(memory_space=pl.ANY)
-    updated, smoothed = pl.pallas_call(
+    held = pl.pallas_call(
         kernel,
-        out_shape=(pltpu.VMEM(weights.shape, f32), pltpu.VMEM(shadow.shape, f32)),
+        out_shape=(
+            pltpu.VMEM((LAYERS, unit // 2, ff), f32),
+            pltpu.VMEM(weights.shape, f32),
+            pltpu.VMEM(shadow.shape, f32),
+            pltpu.VMEM((2 * LAYERS, 128), f32),
+        ),
         in_specs=[hbm] * 5,
-        out_specs=(vmem, vmem),
+        out_specs=(vmem,) * 4,
         scratch_shapes=[
             pltpu.VMEM((LAYERS, BLOCKS, rows, wide_z), f32),
             pltpu.VMEM((LAYERS, BLOCKS, rows, wide_y), f32),
@@ -559,13 +574,10 @@
             pltpu.VMEM((LAYERS, tokens, ff // 2), bf16),
             pltpu.VMEM(acts.shape, bf16),
             pltpu.VMEM(counts.shape, counts.dtype),
-            pltpu.VMEM(weights.shape, f32),
-            pltpu.VMEM(shadow.shape, f32),
             pltpu.VMEM((LAYERS, tokens, rows), f32),
             pltpu.VMEM((LAYERS, tokens, rows), f32),
             pltpu.VMEM((rows, 2 * tokens), f32),
             pltpu.VMEM((LAYERS, rows, 2 * tokens), bf16),
-            pltpu.VMEM((LAYERS, unit // 2, ff), f32),
             pltpu.VMEM((4, LAYERS, 128), f32),
             pltpu.VMEM((3, LAYERS, 128), f32),
             pltpu.VMEM((2 * LAYERS, 128), f32),
@@ -592,16 +604,17 @@
             dma((2,)),
         ],
         compiler_params=pltpu.CompilerParams(
-            collective_id=0, has_side_effects=True, vmem_limit_bytes=58 * 1024 * 1024
+            collective_id=0, has_side_effects=True, vmem_limit_bytes=56 * 1024 * 1024
         ),
     )(acts, og, counts, weights, shadow)
     return pl.pallas_call(
-        writer,
+        update,
         out_shape=(jax.ShapeDtypeStruct(weights.shape, f32), jax.ShapeDtypeStruct(shadow.shape, f32)),
-        in_specs=[vmem, vmem],
+        in_specs=[vmem] * 4,
         out_specs=(hbm, hbm),
-        scratch_shapes=[dma((2, LAYERS))],
-    )(*(pltpu.with_memory_space_constraint(a, pltpu.VMEM) for a in (updated, smoothed)))
+        scratch_shapes=[pltpu.VMEM(weights.shape, f32), pltpu.VMEM(shadow.shape, f32), dma((2, LAYERS, 2))],
+        compiler_params=pltpu.CompilerParams(vmem_limit_bytes=4 * 1024 * 1024),
+    )(*(pltpu.with_memory_space_constraint(a, pltpu.VMEM) for a in held))
 
 
 def solution(mesh):

time: 123 us -> 122 us (level)
  Pallas kernels: 123 us -> 121 us
where the time goes in v8:
time: 122 us
  Pallas kernels  121 us (99%)
    pallas_call x1, Pallas kernels, on_device(): pl.pallas_call(kernel, out_shape=(pltpu.VMEM((LAYERS, unit // 2, ff), f32...  120 us

profile of v8, /device:TPU:1, one launch (start us, length us, event | category | flops | bytes accessed | tf_op | source)
XLA Modules:
  0.0 122.1 jit_solution(6790887402323963810)
XLA Ops:
  0.6 119.9 %shard_map.68 = (f32[2,8,14336]{2,1,0:T(8,128)S(1)}, f32[2,1,8,14336]{3,2,1,0:T(8,128)S(1)}, f32[2,1,8,14336]{3,2,1,0:T(8,128)S(1)}, f32[4,128]{1,0:T(4,128)S(1)}) custom-call(bf16[2,128,256]{2,1,0:T(8,128)(2,1)} %bitcast.3, bf16[2,128,14336]{2,1,0:T(8,128)(2,1)} %bitcast.2, s32[2,1,8]{2,1,0:T(1,128)} %counts_in.1, f32[2,1,8,14336]{3,2,1,0:T(8,128)} %weights.1, ...), custom_call_target="tpu_custom_call" | custom-call | tf_op jit(solution)/shard_map/pallas_call | solution.py:550
  120.6 1.5 %shard_map.69 = (f32[2,1,8,14336]{3,2,1,0:T(8,128)}, f32[2,1,8,14336]{3,2,1,0:T(8,128)}) custom-call(f32[2,8,14336]{2,1,0:T(8,128)S(1)} %get-tuple-element.6.summed, f32[2,1,8,14336]{3,2,1,0:T(8,128)S(1)} %get-tuple-element.7.weights, f32[2,1,8,14336]{3,2,1,0:T(8,128)S(1)} %get-tuple-element.8.shadow, f32[4,128]{1,0:T(4,128)S(1)} %get-tuple-element.9.scalars), custom_call_target="tpu_custom_call" | custom-call | tf_op jit(solution)/shard_map/pallas_call | solution.py:610

commit v9 on v8

--- a/solution.py
+++ b/solution.py
@@ -422,7 +422,7 @@
     z_last(0)
     c_next(0)
     steps(Z, 1, 0, 8, 1)
-    y_units(1, 1, y_first, 0, (0, 1, 2))
+    y_units(1, 1, y_first, 0, (0, 1))
     y_forward(1, 0)
     steps(Z, 1, 0, 8, 2)
     c_next(1)
@@ -432,20 +432,23 @@
     y_begin(0, 1)
     z_last(1)
     steps(Y, 0, 0, 4, 1)
-    y_units_wait(1, 1, 0, 6)
-    y_units(1, 1, y_second, 0, (0, 1, 2))
-    y_units(1, 1, y_first, 1, (3, 4))
-    for layer in range(LAYERS):
-        loop(0, BLOCKS, lambda j: z_copy(layer, j).start())
+    y_units_wait(1, 1, 0, 4)
+    y_units(1, 1, y_second, 0, (0, 1))
+    y_units(1, 1, y_first, 1, (2,))
+    y_units(1, 1, y_first, 2, (3, 4))
     steps(Y, 0, 0, 4, 2)
     steps(Y, 0, 0, 2, 3)
     y_begin(1, 0)
     y_units_add(1, 1, 0)
     starts(YH, 1, 0, 4)
     steps(Y, 1, 0, 2, 1)
+    y_units_wait(1, 1, 1, 2)
+    y_units(1, 1, y_second, 0, (2,))
+    for layer in range(LAYERS):
+        loop(0, BLOCKS, lambda j: z_copy(layer, j).start())
     y_units_add(1, 1, 1)
     steps(YH, 1, 0, 4, 1)
-    y_units_wait(1, 1, 1, 2)
+    y_units_wait(1, 1, 2, 2)
     y_units(1, 1, y_second, 0, (3, 4))
     steps(Y, 1, 0, 2, 2)
     y_units_add(1, 1, 2)
@@ -594,7 +597,7 @@
             dma((2,)),
             dma((LAYERS, 2)),
             dma((LAYERS, 2)),
-            dma((2,)),
+            dma((3,)),
             dma((5,)),
             dma((2,)),
             dma((LAYERS,)),

time: 122 us -> 121 us (level)
  no operation moved by 1% of the time
where the time goes in v9:
time: 121 us
  Pallas kernels  121 us (100%)
    pallas_call x1, Pallas kernels, on_device(): pl.pallas_call(kernel, out_shape=(pltpu.VMEM((LAYERS, unit // 2, ff), f32...  119 us

profile of v9, /device:TPU:1, one launch (start us, length us, event | category | flops | bytes accessed | tf_op | source)
XLA Modules:
  0.0 121.4 jit_solution(1881005339789231086)
XLA Ops:
  0.6 119.2 %shard_map.68 = (f32[2,8,14336]{2,1,0:T(8,128)S(1)}, f32[2,1,8,14336]{3,2,1,0:T(8,128)S(1)}, f32[2,1,8,14336]{3,2,1,0:T(8,128)S(1)}, f32[4,128]{1,0:T(4,128)S(1)}) custom-call(bf16[2,128,256]{2,1,0:T(8,128)(2,1)} %bitcast.3, bf16[2,128,14336]{2,1,0:T(8,128)(2,1)} %bitcast.2, s32[2,1,8]{2,1,0:T(1,128)} %counts_in.1, f32[2,1,8,14336]{3,2,1,0:T(8,128)} %weights.1, ...), custom_call_target="tpu_custom_call" | custom-call | tf_op jit(solution)/shard_map/pallas_call | solution.py:553
  119.9 1.5 %shard_map.69 = (f32[2,1,8,14336]{3,2,1,0:T(8,128)}, f32[2,1,8,14336]{3,2,1,0:T(8,128)}) custom-call(f32[2,8,14336]{2,1,0:T(8,128)S(1)} %get-tuple-element.6.summed, f32[2,1,8,14336]{3,2,1,0:T(8,128)S(1)} %get-tuple-element.7.weights, f32[2,1,8,14336]{3,2,1,0:T(8,128)S(1)} %get-tuple-element.8.shadow, f32[4,128]{1,0:T(4,128)S(1)} %get-tuple-element.9.scalars), custom_call_target="tpu_custom_call" | custom-call | tf_op jit(solution)/shard_map/pallas_call | solution.py:613

commit v10 on v9

--- a/solution.py
+++ b/solution.py
@@ -437,8 +437,8 @@
     y_units(1, 1, y_first, 1, (2,))
     y_units(1, 1, y_first, 2, (3, 4))
     steps(Y, 0, 0, 4, 2)
+    y_begin(1, 0)
     steps(Y, 0, 0, 2, 3)
-    y_begin(1, 0)
     y_units_add(1, 1, 0)
     starts(YH, 1, 0, 4)
     steps(Y, 1, 0, 2, 1)

time: 121 us -> 121 us (level)
  no operation moved by 1% of the time
where the time goes in v10:
time: 121 us
  Pallas kernels  121 us (100%)
    pallas_call x1, Pallas kernels, on_device(): pl.pallas_call(kernel, out_shape=(pltpu.VMEM((LAYERS, unit // 2, ff), f32...  119 us

profile of v10, /device:TPU:1, one launch (start us, length us, event | category | flops | bytes accessed | tf_op | source)
XLA Modules:
  0.0 121.4 jit_solution(7094772202810458516)
XLA Ops:
  0.6 119.2 %shard_map.68 = (f32[2,8,14336]{2,1,0:T(8,128)S(1)}, f32[2,1,8,14336]{3,2,1,0:T(8,128)S(1)}, f32[2,1,8,14336]{3,2,1,0:T(8,128)S(1)}, f32[4,128]{1,0:T(4,128)S(1)}) custom-call(bf16[2,128,256]{2,1,0:T(8,128)(2,1)} %bitcast.3, bf16[2,128,14336]{2,1,0:T(8,128)(2,1)} %bitcast.2, s32[2,1,8]{2,1,0:T(1,128)} %counts_in.1, f32[2,1,8,14336]{3,2,1,0:T(8,128)} %weights.1, ...), custom_call_target="tpu_custom_call" | custom-call | tf_op jit(solution)/shard_map/pallas_call | solution.py:553
  119.9 1.5 %shard_map.69 = (f32[2,1,8,14336]{3,2,1,0:T(8,128)}, f32[2,1,8,14336]{3,2,1,0:T(8,128)}) custom-call(f32[2,8,14336]{2,1,0:T(8,128)S(1)} %get-tuple-element.6.summed, f32[2,1,8,14336]{3,2,1,0:T(8,128)S(1)} %get-tuple-element.7.weights, f32[2,1,8,14336]{3,2,1,0:T(8,128)S(1)} %get-tuple-element.8.shadow, f32[4,128]{1,0:T(4,128)S(1)} %get-tuple-element.9.scalars), custom_call_target="tpu_custom_call" | custom-call | tf_op jit(solution)/shard_map/pallas_call | solution.py:613

commit v11 on v10

--- a/solution.py
+++ b/solution.py
@@ -444,12 +444,13 @@
     steps(Y, 1, 0, 2, 1)
     y_units_wait(1, 1, 1, 2)
     y_units(1, 1, y_second, 0, (2,))
-    for layer in range(LAYERS):
-        loop(0, BLOCKS, lambda j: z_copy(layer, j).start())
+    loop(0, BLOCKS, lambda j: z_copy(0, j).start())
     y_units_add(1, 1, 1)
     steps(YH, 1, 0, 4, 1)
     y_units_wait(1, 1, 2, 2)
-    y_units(1, 1, y_second, 0, (3, 4))
+    y_units(1, 1, y_second, 0, (3,))
+    loop(0, BLOCKS, lambda j: z_copy(1, j).start())
+    y_units(1, 1, y_second, 0, (4,))
     steps(Y, 1, 0, 2, 2)
     y_units_add(1, 1, 2)
     steps(YH, 1, 0, 4, 2)

time: 121 us -> 121 us (level)
  no operation moved by 1% of the time
where the time goes in v11:
time: 121 us
  Pallas kernels  121 us (100%)
    pallas_call x1, Pallas kernels, on_device(): pl.pallas_call(kernel, out_shape=(pltpu.VMEM((LAYERS, unit // 2, ff), f32...  119 us

profile of v11, /device:TPU:1, one launch (start us, length us, event | category | flops | bytes accessed | tf_op | source)
XLA Modules:
  0.0 121.4 jit_solution(8027091909348284993)
XLA Ops:
  0.6 119.2 %shard_map.68 = (f32[2,8,14336]{2,1,0:T(8,128)S(1)}, f32[2,1,8,14336]{3,2,1,0:T(8,128)S(1)}, f32[2,1,8,14336]{3,2,1,0:T(8,128)S(1)}, f32[4,128]{1,0:T(4,128)S(1)}) custom-call(bf16[2,128,256]{2,1,0:T(8,128)(2,1)} %bitcast.3, bf16[2,128,14336]{2,1,0:T(8,128)(2,1)} %bitcast.2, s32[2,1,8]{2,1,0:T(1,128)} %counts_in.1, f32[2,1,8,14336]{3,2,1,0:T(8,128)} %weights.1, ...), custom_call_target="tpu_custom_call" | custom-call | tf_op jit(solution)/shard_map/pallas_call | solution.py:554
  119.9 1.5 %shard_map.69 = (f32[2,1,8,14336]{3,2,1,0:T(8,128)}, f32[2,1,8,14336]{3,2,1,0:T(8,128)}) custom-call(f32[2,8,14336]{2,1,0:T(8,128)S(1)} %get-tuple-element.6.summed, f32[2,1,8,14336]{3,2,1,0:T(8,128)S(1)} %get-tuple-element.7.weights, f32[2,1,8,14336]{3,2,1,0:T(8,128)S(1)} %get-tuple-element.8.shadow, f32[4,128]{1,0:T(4,128)S(1)} %get-tuple-element.9.scalars), custom_call_target="tpu_custom_call" | custom-call | tf_op jit(solution)/shard_map/pallas_call | solution.py:614
